TPU v7x, 256 devices: a whole 4x4x8 slice. The times are simulated.
256 devices in a mesh: dp: 32 (over y, z), tensor: 8 (over x, core).
Axes of the slice: x: 4, y: 4, z: 8, core: 2. Of those that a mesh axis runs over, the one named last changes fastest.
Arguments:
- query: bfloat16 [256, 64, 128], P('dp', 'tensor'), may hold values from -8 to 8
- kv_pages: bfloat16 [2816, 8, 2, 128, 128], P('dp', 'tensor'), may hold values from -8 to 8
- move_plan: int32 [32, 3, 48], P('dp'), may hold values from 0 to 87, as said below
- move_count: int32 [32], P('dp'), may hold values from 36 to 48
- block_table: int32 [256, 8], P('dp'), may hold values from 0 to 87, as said below
- seq_lens: int32 [256], P('dp'), may hold values from 1 to 1024
- out_weight: bfloat16 [8192, 8192], P('tensor', 'dp'), may hold values from -0.0625 to 0.0625
Outputs:
- new_pages: bfloat16 [2816, 8, 2, 128, 128], P('dp', 'tensor')
- projected: bfloat16 [256, 8192], P(None, 'dp')
Inputs may be any that keep to these rules, and one draw needn't show every extreme that they name: `move_plan`: row 0 holds the device's own source slots, distinct within a device; row 1 target devices; row 2 target slots. Entries at or past the device's move_count are padding to be ignored. At most 2 valid moves go from one device to one device, and some pair has exactly 2. The (target device, target slot) pairs of all valid moves are distinct. `block_table`: all entries of the sequences of one device are distinct slots of that device; sequence s belongs to device s // 8.
All inputs are finite; a program needn't handle non-finite values.
Results may differ from a plain program's by a relative error of at most 0.0055.
Values may be sent and summed in bfloat16 or wider, within the bound.
A program may use at most 64 MiB of HBM per device.

v0:
```python
import math

import jax
import jax.numpy as jnp
from jax import lax
from jax.sharding import PartitionSpec as P

HD = 128
BLOCK = 128
BLOCKS = 8
CAP = 2


def laid_out(pieces, dim):
    shape = list(pieces.shape[1:])
    shape[dim] *= pieces.shape[0]
    return jnp.moveaxis(pieces, 0, dim).reshape(shape)


def copy_for_each(array, axis):
    copies = jnp.broadcast_to(array, (lax.axis_size(axis), *array.shape))
    return lax.all_to_all(copies, axis, split_axis=0, concat_axis=0, tiled=True)


def gather_directly(array, axis, dim):
    return laid_out(copy_for_each(array, axis), dim)


def taken_together(array, axis):
    everything = copy_for_each(array, axis)
    return jnp.sum(everything, axis=0)


def body(query, kv_pages, move_plan, move_count, block_table, seq_lens, out_weight):
    slots_here = kv_pages.shape[0]
    move_total = move_plan.shape[2]
    devices = lax.axis_size("dp")
    capacity = CAP
    holding_rows = devices * capacity
    move_list = move_plan[0]
    move_index = jnp.arange(move_total, dtype=jnp.int32)
    is_valid = move_index < move_count[0]
    target_dev = move_list[1]
    earlier = (
        (target_dev[:, None] == target_dev[None, :])
        & is_valid[None, :]
        & (move_index[None, :] < move_index[:, None])
    )
    dest_rank = jnp.sum(earlier.astype(jnp.int32), axis=1)
    send_row = jnp.where(is_valid, target_dev * capacity + dest_rank, -1)
    flat_pages = kv_pages.reshape(slots_here, -1)
    picked = flat_pages[move_list[0]]
    select = jnp.arange(holding_rows, dtype=jnp.int32)[:, None] == send_row[None, :]
    outgoing = jnp.dot(
        select.astype(jnp.bfloat16), picked, preferred_element_type=jnp.float32
    ).astype(jnp.bfloat16)
    outgoing = outgoing.reshape((holding_rows,) + kv_pages.shape[1:])
    out_slots = jnp.sum(select.astype(jnp.int32) * (move_list[2][None, :] + 1), axis=1) - 1
    slot_tags = out_slots.astype(jnp.float32).astype(jnp.bfloat16)
    arrived, arrived_tags = (
        lax.all_to_all(outgoing, "dp", split_axis=0, concat_axis=0, tiled=True),
        lax.all_to_all(slot_tags, "dp", split_axis=0, concat_axis=0, tiled=True),
    )
    incoming = arrived_tags.astype(jnp.float32).astype(jnp.int32)
    hit_table = jnp.arange(slots_here, dtype=jnp.int32)[:, None] == incoming[None, :]
    placed = jnp.dot(
        hit_table.astype(jnp.bfloat16),
        arrived.reshape(holding_rows, -1),
        preferred_element_type=jnp.float32,
    ).astype(jnp.bfloat16)
    written = jnp.any(hit_table, axis=1)
    new_pages = jnp.where(written[:, None], placed, flat_pages).reshape(kv_pages.shape)
    seq_here = query.shape[0]
    local_heads = new_pages.shape[1]
    head_dim = query.shape[2]
    group_size = query.shape[1] // local_heads
    context = BLOCKS * BLOCK
    gathered = new_pages[block_table]
    key_rows = jnp.transpose(gathered[:, :, :, 0], (0, 2, 1, 3, 4)).reshape(
        seq_here, local_heads, context, head_dim
    )
    value_rows = jnp.transpose(gathered[:, :, :, 1], (0, 2, 1, 3, 4)).reshape(
        seq_here, local_heads, context, head_dim
    )
    grouped = query.reshape(seq_here, local_heads, group_size, head_dim)
    score_scale = 1.0 / math.sqrt(HD)
    scores = (
        jnp.einsum("skgd,sktd->skgt", grouped, key_rows, preferred_element_type=jnp.float32)
        * score_scale
    )
    position = jnp.arange(context, dtype=jnp.int32)
    scores = jnp.where(position[None, None, None, :] < seq_lens[:, None, None, None], scores, -1e30)
    largest = jnp.max(scores, axis=-1, keepdims=True)
    expo = jnp.exp(scores - largest)
    weights = (expo / jnp.sum(expo, axis=-1, keepdims=True)).astype(jnp.bfloat16)
    mixed_heads = jnp.einsum(
        "skgt,sktd->skgd", weights, value_rows, preferred_element_type=jnp.float32
    )
    attention = mixed_heads.reshape(seq_here, local_heads * group_size * head_dim).astype(
        jnp.bfloat16
    )
    partial_sums = jnp.dot(
        gather_directly(attention, "dp", 0), out_weight, preferred_element_type=jnp.float32
    )
    summed = taken_together(partial_sums, "tensor")
    return (new_pages, summed.astype(jnp.bfloat16))


def solution(mesh):
    placed = (
        P("dp", "tensor", None),
        P("dp", "tensor", None, None, None),
        P("dp", None, None),
        P("dp"),
        P("dp", None),
        P("dp"),
        P("tensor", "dp"),
    )
    return jax.shard_map(
        body,
        mesh=mesh,
        in_specs=placed,
        out_specs=(P("dp", "tensor", None, None, None), P(None, "dp")),
        check_vma=False,
    )
```

profile of v0, /device:TPU:1, one launch (start us, length us, event | category | flops | bytes accessed | tf_op | source)
XLA Modules:
  0.0 230.5 jit_solution(2770679672338814188)
XLA Ops:
  0.6 0.0 copy-start
  0.6 0.7 add_bitcast_fusion
  2.0 0.2 convert_reduce_fusion
  2.2 0.7 add_select_fusion
  2.9 0.1 select_reduce_fusion
  3.0 0.7 convert_element_type.80
  3.7 12.0 %all-to-all-start = ((bf16[32,2,1]{1,2,0:T(2,128)(2,1)}), bf16[32,2,1]{1,2,0:T(2,128)(2,1)S(1)}, u32[]{:S(2)}, u32[]{:S(2)}) async-start(bf16[32,2,1]{1,2,0:T(2,128)(2,1)} %convert_element_type.80), calls=%async_computation | async-start | bytes 32768 | tf_op jit(solution)/shard_map/all_to_all | solution.py:62
  15.8 0.7 fusion.20
  16.4 9.5 %copy.43 = bf16[11,8,256,128]{3,1,2,0:T(8,128)(2,1)} copy(bf16[11,8,256,128]{3,2,1,0:T(8,128)(2,1)} %bitcast.69) | data formatting | bytes 11534336
  25.9 10.3 %gather_fusion = bf16[48,32768]{1,0:T(8,128)(2,1)} fusion(bf16[88,32768]{1,0:T(8,128)(2,1)} %bitcast.68, s32[1024]{0:T(1024)S(1)} %pad_clamp_fusion.1), kind=kCustom, calls=%fused_computation | custom fusion | bytes 6291648 | tf_op jit(solution)/shard_map/gather | solution.py:52
  36.2 3.2 %fusion.7 = bf16[8,8,256,128]{3,1,2,0:T(8,128)(2,1)S(1)} fusion(bf16[48,32768]{1,0:T(8,128)(2,1)} %gather_fusion, s32[48]{0:T(128)S(1)} %add_select_fusion), kind=kOutput, calls=%fused_computation.10 | convolution fusion | flops 203426816 | bytes 7340224 | tf_op jit(solution)/shard_map/dot_general | solution.py:54
  39.4 3.2 %copy.28 = bf16[8,8,256,128]{3,2,1,0:T(8,128)(2,1)} copy(bf16[8,8,256,128]{3,1,2,0:T(8,128)(2,1)S(1)} %fusion.7) | data formatting | bytes 8388608
  42.6 0.0 all-to-all-done
  42.6 0.0 copy-start.2
  42.6 0.0 copy-start.3
  42.6 9.5 %all-to-all-start.1 = ((bf16[64,1,2,128,128]{4,3,2,1,0:T(8,128)(2,1)}), bf16[64,1,2,128,128]{4,3,2,1,0:T(8,128)(2,1)}, u32[]{:S(2)}, u32[]{:S(2)}) async-start(bf16[64,1,2,128,128]{4,3,2,1,0:T(8,128)(2,1)} %bitcast.73), calls=%async_computation.1 | async-start | bytes 8388608 | tf_op jit(solution)/shard_map/all_to_all | solution.py:61
  52.1 0.0 copy-done.2
  52.1 0.1 reshape.186
  52.2 0.0 copy-done.3
  52.2 0.1 iota_compare_fusion
  52.3 0.1 convert_reduce_fusion.1
  52.4 0.1 convert_element_type.73
  52.5 0.1 fusion.16
  52.6 93.9 %all-to-all-done.1 = bf16[64,1,2,128,128]{4,3,2,1,0:T(8,128)(2,1)} async-done(((bf16[64,1,2,128,128]{4,3,2,1,0:T(8,128)(2,1)}), bf16[64,1,2,128,128]{4,3,2,1,0:T(8,128)(2,1)}, u32[]{:S(2)}, u32[]{:S(2)}) %all-to-all-start.1) | async-done | bytes 4194336 | tf_op jit(solution)/shard_map/all_to_all | solution.py:61
  146.4 10.4 %fusion.4 = bf16[11,8,256,128]{3,1,2,0:T(8,128)(2,1)S(1)} fusion(bf16[8,8,256,128]{3,2,1,0:T(8,128)(2,1)} %bitcast.24, pred[88]{0:T(512)(128)(4,1)S(1)} %fusion.16, s32[64]{0:T(128)S(1)} %convert_element_type.73, bf16[11,8,256,128]{3,2,1,0:T(8,128)(2,1)} %bitcast.70), kind=kOutput, calls=%fused_computation.9 | convolution fusion | flops 374871552 | bytes 15728984 | tf_op jit(solution)/shard_map/dot_general | solution.py:66
  156.9 4.2 %copy.30 = bf16[11,8,256,128]{3,2,1,0:T(8,128)(2,1)} copy(bf16[11,8,256,128]{3,1,2,0:T(8,128)(2,1)S(1)} %fusion.4) | data formatting | bytes 11534336
  161.0 5.6 %gather_fusion.1 = bf16[64,2,128,128]{3,2,1,0:T(8,128)(2,1)} fusion(bf16[88,2,128,128]{3,2,1,0:T(8,128)(2,1)} %bitcast.71, s32[1024]{0:T(1024)S(1)} %pad_clamp_fusion), kind=kCustom, calls=%fused_computation.1 | custom fusion | bytes 8388864 | tf_op jit(solution)/shard_map/gather | solution.py:78
  166.7 0.0 copy-start.1
  166.7 4.0 %fusion.21 = (bf16[8,8,1,1,128,128]{5,4,3,1,0,2:T(8,128)(2,1)}, bf16[8,8,1,1,128,128]{5,4,3,1,0,2:T(8,128)(2,1)S(1)}) fusion(bf16[8,8,1,2,128,128]{5,4,3,1,0,2:T(8,128)(2,1)} %bitcast.74), kind=kLoop, calls=%fused_computation.44 | loop fusion | bytes 8388608 | tf_op jit(solution)/shard_map/slice | solution.py:79
  170.7 0.0 copy-done.1
  170.7 2.4 %fusion.22 = (f32[8,8]{1,0:T(8,128)S(1)}, f32[8,8,1024]{2,1,0:T(8,128)S(1)}) fusion(bf16[8,1024,128]{2,1,0:T(8,128)(2,1)} %bitcast.76, bf16[8,8,128]{2,1,0:T(8,128)(2,1)S(1)} %copy-done.1, pred[8,1024]{1,0:T(8,128)(4,1)S(1)} %iota_compare_fusion), kind=kOutput, calls=%fused_computation.45 | convolution fusion | flops 17040384 | bytes 2384128 | tf_op jit(solution)/shard_map/sub | solution.py:94
  173.1 0.4 fusion.12
  173.6 0.1 broadcast_in_dim.51
  173.6 21.8 %all_to_all.21 = bf16[32,8,1024]{2,1,0:T(8,128)(2,1)S(1)} all-to-all(bf16[32,8,1024]{2,1,0:T(8,128)(2,1)S(1)} %broadcast_in_dim.51), channel_id=1, replica_groups=mesh['dp'=32,'tensor'=8] {'dp'}, dimensions={0} | all-to-all | bytes 1048576 | tf_op jit(solution)/shard_map/all_to_all | solution.py:22
  195.4 0.0 copy-done
  195.4 0.3 fusion.13
  195.7 0.2 broadcast_in_dim.52
  195.9 33.8 %all_to_all.22 = f32[8,256,256]{2,1,0:T(8,128)S(1)} all-to-all(f32[8,256,256]{2,1,0:T(8,128)S(1)} %broadcast_in_dim.52), channel_id=1, replica_groups=mesh['dp'=32,'tensor'=8] {'tensor'}, dimensions={0} | all-to-all | bytes 4194304 | tf_op jit(solution)/shard_map/all_to_all | solution.py:22
  229.7 0.8 reduce_sum.39
  (6 shorter events, 0.0 us)
Async XLA Ops:
  0.6 194.8 %copy-start = (bf16[1024,256]{1,0:T(8,128)(2,1)S(1)}, bf16[1024,256]{1,0:T(8,128)(2,1)}, u32[]{:S(2)}) copy-start(bf16[1024,256]{1,0:T(8,128)(2,1)} %param.13) | copy-start | bytes 1572868
  3.7 38.9 %all-to-all-start = ((bf16[32,2,1]{1,2,0:T(2,128)(2,1)}), bf16[32,2,1]{1,2,0:T(2,128)(2,1)S(1)}, u32[]{:S(2)}, u32[]{:S(2)}) async-start(bf16[32,2,1]{1,2,0:T(2,128)(2,1)} %convert_element_type.80), calls=%async_computation | async-start | bytes 32768 | tf_op jit(solution)/shard_map/all_to_all | solution.py:62
  42.6 9.5 %copy-start.2 = (s32[8,8]{1,0:T(8,128)S(1)}, s32[8,8]{1,0:T(8,128)}, u32[]{:S(2)}) copy-start(s32[8,8]{1,0:T(8,128)} %param.11) | copy-start | bytes 772
  42.6 9.6 %copy-start.3 = (s32[8]{0:T(128)S(1)}, s32[8]{0:T(128)}, u32[]{:S(2)}) copy-start(s32[8]{0:T(128)} %param.12) | copy-start | bytes 100
  42.6 103.8 %all-to-all-start.1 = ((bf16[64,1,2,128,128]{4,3,2,1,0:T(8,128)(2,1)}), bf16[64,1,2,128,128]{4,3,2,1,0:T(8,128)(2,1)}, u32[]{:S(2)}, u32[]{:S(2)}) async-start(bf16[64,1,2,128,128]{4,3,2,1,0:T(8,128)(2,1)} %bitcast.73), calls=%async_computation.1 | async-start | bytes 8388608 | tf_op jit(solution)/shard_map/all_to_all | solution.py:61
  166.7 4.0 %copy-start.1 = (bf16[8,8,128]{2,1,0:T(8,128)(2,1)S(1)}, bf16[8,8,128]{2,1,0:T(8,128)(2,1)}, u32[]{:S(2)}) copy-start(bf16[8,8,128]{2,1,0:T(8,128)(2,1)} %param.7) | copy-start | bytes 49156
where the time goes:
time: 231 us
  waiting for transfers between devices  93.9 us (41%)
  blocking collectives  55.6 us (24%)
  local copies, waits for them, and re-layouts  37.9 us (16%)
  starting transfers between devices  21.5 us (9%)
  matrix products  16.8 us (7%)
  other arithmetic  3.4 us (1%)
    all_to_all x1, waiting for transfers between devices, body(): lax.all_to_all(outgoing, 'dp', split_axis=0, concat_axis=0, tiled=True)  93.9 us
    all_to_all x2, blocking collectives, copy_for_each(): return lax.all_to_all(copies, axis, split_axis=0, concat_axis=0, tiled=True)  55.6 us
    unnamed x12, local copies, waits for them, and re-layouts  16.9 us
    all_to_all x1, starting transfers between devices, body(): lax.all_to_all(slot_tags, 'dp', split_axis=0, concat_axis=0, tiled=True)  12 us
    dot_general x1, matrix products, body(): jnp.dot(hit_table.astype(jnp.bfloat16), arrived.reshape(holding_rows, -1)...  10.4 us
    gather x1, local copies, waits for them, and re-layouts, body(): picked = flat_pages[move_list[0]]  10.3 us
    all_to_all x1, starting transfers between devices, body(): lax.all_to_all(outgoing, 'dp', split_axis=0, concat_axis=0, tiled=True)  9.49 us
    gather x1, local copies, waits for them, and re-layouts, body(): gathered = new_pages[block_table]  5.64 us
  transfers between devices with their start and end apart: 2, of which 1 were waited for; matrix products, arithmetic and copies ran while one was open for 12% of the time, Pallas kernels for 0%

commit v1 on v0

v1 whole, which is shorter than its diff:
```python
import functools
import math

import jax
import jax.numpy as jnp
from jax import lax
from jax.experimental import pallas as pl
from jax.experimental.pallas import tpu as pltpu
from jax.sharding import PartitionSpec as P

HD = 128
BLOCK = 128
BLOCKS = 8
CAP = 2
SLOTS = 88
MOVES = 48
NY, NZ = 4, 8
NDP = NY * NZ
NT = 8
SEQ_DEV = 8
MESH = pl.DeviceIdType.MESH
VMEM_LIMIT = 60 * 1024 * 1024
PAGE = (2, BLOCK, HD)
SHIFTS = [(dy, dz) for dy in range(NY) for dz in range(NZ)]


def far(shift):
    return min(shift[0], NY - shift[0]) + min(shift[1], NZ - shift[1])


def vspec():
    return pl.BlockSpec(memory_space=pltpu.VMEM)


def sspec():
    return pl.BlockSpec(memory_space=pltpu.SMEM)


def aspec():
    return pl.BlockSpec(memory_space=pl.ANY)


def pack_kernel(plan_ref, count_ref, kv_ref, send_ref, tags_ref, used, sems):
    me = lax.axis_index("dp")
    y, z = me // NZ, me % NZ
    for k in range(NDP):
        used[k] = 0
    count = count_ref[0]
    rows = lax.broadcasted_iota(jnp.int32, (NDP, 128), 0)
    cols = lax.broadcasted_iota(jnp.int32, (NDP, 128), 1)

    def step(m, tags):
        valid = m < count
        target = plan_ref[1, m]
        shift = lax.rem(target // NZ - y + NY, NY) * NZ + lax.rem(target % NZ - z + NZ, NZ)
        rank = used[shift]

        @pl.when(valid)
        def _():
            used[shift] = rank + 1
            pltpu.make_async_copy(
                kv_ref.at[plan_ref[0, m]], send_ref.at[shift * CAP + rank], sems.at[m]
            ).start()

        hit = (rows == shift) & (cols == rank) & valid
        return jnp.where(hit, plan_ref[2, m], tags)

    tags = lax.fori_loop(0, MOVES, step, jnp.full((NDP, 128), -1, jnp.int32))
    tags_ref[...] = tags.reshape(NDP, 1, 128)

    def drain(m, carry):
        @pl.when(m < count)
        def _():
            pltpu.make_async_copy(kv_ref.at[0], send_ref.at[0], sems.at[m]).wait()

        return carry

    lax.fori_loop(0, MOVES, drain, 0)


def exchange_kernel(send_ref, tags_ref, kv_ref, comb_ref, got_ref, load_sem, send_sem, recv_sem, tag_send, tag_recv):
    me = lax.axis_index("dp")
    t = lax.axis_index("tensor")
    y, z = me // NZ, me % NZ
    load = pltpu.make_async_copy(kv_ref, comb_ref.at[pl.ds(0, SLOTS)], load_sem)
    load.start()
    bar = pltpu.get_barrier_semaphore()
    order = sorted([s for s in SHIFTS if s != (0, 0)], key=lambda s: -far(s))
    peer = {}
    for dy, dz in order:
        peer[dy, dz] = lax.rem(y + dy, NY) * NZ + lax.rem(z + dz, NZ)
        pl.semaphore_signal(bar, inc=1, device_id=(peer[dy, dz], t), device_id_type=MESH)
    pl.semaphore_wait(bar, len(order))
    copies = []
    for dy, dz in order:
        k = dy * NZ + dz
        copy = pltpu.make_async_remote_copy(
            src_ref=send_ref.at[pl.ds(k * CAP, CAP)],
            dst_ref=comb_ref.at[pl.ds(SLOTS + k * CAP, CAP)],
            send_sem=send_sem.at[k],
            recv_sem=recv_sem.at[k],
            device_id=(peer[dy, dz], t),
            device_id_type=MESH,
        )
        copy.start()
        copies.append(copy)
        copy = pltpu.make_async_remote_copy(
            src_ref=tags_ref.at[k],
            dst_ref=got_ref.at[k],
            send_sem=tag_send.at[k],
            recv_sem=tag_recv.at[k],
            device_id=(peer[dy, dz], t),
            device_id_type=MESH,
        )
        copy.start()
        copies.append(copy)
    got_ref[0] = tags_ref[0]
    comb_ref[SLOTS : SLOTS + CAP] = send_ref[0:CAP]
    load.wait()
    for copy in copies:
        copy.wait()


def attend_kernel(got_ref, table_ref, lens_ref, query_ref, comb_ref, new_ref, att_ref, where_ref, mixed, sems):
    for s in range(SLOTS):
        where_ref[s] = s
    for k in range(NDP):
        for c in range(CAP):
            slot = got_ref[k, c]

            @pl.when(slot >= 0)
            def _():
                where_ref[slot] = SLOTS + k * CAP + c

    copies = []
    for s in range(SLOTS):
        copy = pltpu.make_async_copy(comb_ref.at[where_ref[s]], new_ref.at[s], sems.at[s])
        copy.start()
        copies.append(copy)
    position = lax.broadcasted_iota(jnp.int32, (8, BLOCKS * BLOCK), 1)
    for s in range(SEQ_DEV):
        at = [where_ref[table_ref[s, b]] for b in range(BLOCKS)]
        keys = jnp.concatenate([comb_ref[i, 0] for i in at], axis=0)
        scores = lax.dot_general(
            query_ref[s], keys, (((1,), (1,)), ((), ())), preferred_element_type=jnp.float32
        ) * (1.0 / math.sqrt(HD))
        scores = jnp.where(position < lens_ref[s], scores, -1e30)
        expo = jnp.exp(scores - jnp.max(scores, axis=1, keepdims=True))
        weights = (expo / jnp.sum(expo, axis=1, keepdims=True)).astype(jnp.bfloat16)
        values = jnp.concatenate([comb_ref[i, 1] for i in at], axis=0)
        mixed[s * 8 : s * 8 + 8, :] = jnp.dot(weights, values, preferred_element_type=jnp.float32)
    att_ref[...] = jnp.concatenate(
        [mixed[pl.ds(h, SEQ_DEV, stride=8), :] for h in range(8)], axis=1
    ).astype(jnp.bfloat16)
    for copy in copies:
        copy.wait()


def project_kernel(att_ref, w_ref, out_ref, gath, part, red, z_send, z_recv, y_send, y_recv, r_send, r_recv, o_send, o_recv):
    me = lax.axis_index("dp")
    t = lax.axis_index("tensor")
    y, z = me // NZ, me % NZ
    zs = [lax.rem(z + d, NZ) for d in range(NZ)]
    ys = [lax.rem(y + d, NY) for d in range(NY)]
    ts = [lax.rem(t + d, NT) for d in range(NT)]
    bar = pltpu.get_barrier_semaphore()
    peers = (
        [(y * NZ + zs[d], t) for d in range(1, NZ)]
        + [(ys[d] * NZ + z, t) for d in range(1, NY)]
        + [(me, ts[d]) for d in range(1, NT)]
    )
    for peer in peers:
        pl.semaphore_signal(bar, inc=1, device_id=peer, device_id_type=MESH)
    pl.semaphore_wait(bar, len(peers))

    def remote(src, dst, send, recv, device):
        copy = pltpu.make_async_remote_copy(
            src_ref=src, dst_ref=dst, send_sem=send, recv_sem=recv, device_id=device, device_id_type=MESH
        )
        copy.start()
        return copy

    z_order = sorted(range(1, NZ), key=lambda d: -min(d, NZ - d))
    along_z = {d: remote(att_ref, gath.at[me], z_send.at[d], z_recv.at[d], (y * NZ + zs[d], t)) for d in z_order}
    gath[me] = att_ref[...]
    along_y = []
    for d in range(1, NY):
        along_y.append(remote(att_ref, gath.at[me], y_send.at[d], y_recv.at[d], (ys[d] * NZ + z, t)))
    for e in sorted(range(1, NZ), key=lambda d: min(d, NZ - d)):
        along_z[e].wait_recv()
        held = y * NZ + lax.rem(z - e + NZ, NZ)
        for d in (2, 1, 3):
            n = e * NY + d
            along_y.append(remote(gath.at[held], gath.at[held], y_send.at[n], y_recv.at[n], (ys[d] * NZ + z, t)))
    for copy in along_y:
        copy.wait_recv()
    rows = gath[...].reshape(NDP * SEQ_DEV, 8 * HD)
    part[...] = jnp.dot(rows, w_ref[...], preferred_element_type=jnp.float32)
    chunk = NDP * SEQ_DEV // NT
    t_order = (4, 5, 3, 2, 6, 1, 7)

    def rows_of(i):
        return pl.ds(pl.multiple_of(i * chunk, chunk), chunk)

    sums = [remote(part.at[rows_of(ts[d])], red.at[d], r_send.at[d], r_recv.at[d], (me, ts[d])) for d in t_order]
    total = part[rows_of(t), :]
    for copy in sums:
        copy.wait_recv()
    for d in range(1, NT):
        total = total + red[d]
    out_ref[rows_of(t), :] = total.astype(jnp.bfloat16)
    outs = [
        remote(out_ref.at[rows_of(t)], out_ref.at[rows_of(t)], o_send.at[d], o_recv.at[d], (me, ts[d])) for d in t_order
    ]
    for copy in outs:
        copy.wait_recv()
    for d in range(1, NZ):
        along_z[d].wait_send()
    for copy in along_y + sums + outs:
        copy.wait_send()


def body(query, kv_pages, move_plan, move_count, block_table, seq_lens, out_weight):
    kv = kv_pages.reshape(SLOTS, *PAGE)
    dma = pltpu.SemaphoreType.DMA
    send, tags = pl.pallas_call(
        pack_kernel,
        name="pack",
        out_shape=[pltpu.VMEM((NDP * CAP, *PAGE), jnp.bfloat16), pltpu.VMEM((NDP, 1, 128), jnp.int32)],
        in_specs=[sspec(), sspec(), aspec()],
        out_specs=[vspec(), vspec()],
        scratch_shapes=[pltpu.SMEM((NDP,), jnp.int32), dma((MOVES,))],
        compiler_params=pltpu.CompilerParams(vmem_limit_bytes=VMEM_LIMIT // 2),
    )(move_plan[0], move_count, kv)
    comb, got = pl.pallas_call(
        exchange_kernel,
        name="exchange",
        out_shape=[pltpu.VMEM((SLOTS + NDP * CAP, *PAGE), jnp.bfloat16), pltpu.VMEM((NDP, 1, 128), jnp.int32)],
        in_specs=[vspec(), vspec(), aspec()],
        out_specs=[vspec(), vspec()],
        scratch_shapes=[dma(()), dma((NDP,)), dma((NDP,)), dma((NDP,)), dma((NDP,))],
        compiler_params=pltpu.CompilerParams(
            collective_id=0, has_side_effects=True, vmem_limit_bytes=VMEM_LIMIT // 2
        ),
    )(send, tags, kv)
    new_pages, attention = pl.pallas_call(
        attend_kernel,
        name="attend",
        out_shape=[
            jax.ShapeDtypeStruct((SLOTS, *PAGE), jnp.bfloat16),
            pltpu.VMEM((SEQ_DEV, 8 * HD), jnp.bfloat16),
        ],
        in_specs=[sspec(), sspec(), sspec(), vspec(), vspec()],
        out_specs=[aspec(), vspec()],
        scratch_shapes=[pltpu.SMEM((SLOTS,), jnp.int32), pltpu.VMEM((64, HD), jnp.float32), dma((SLOTS,))],
        compiler_params=pltpu.CompilerParams(vmem_limit_bytes=VMEM_LIMIT // 2),
    )(got.reshape(NDP, 128), block_table, seq_lens, query, comb)
    projected = pl.pallas_call(
        project_kernel,
        name="project",
        out_shape=jax.ShapeDtypeStruct((NDP * SEQ_DEV, out_weight.shape[1]), jnp.bfloat16),
        in_specs=[vspec(), vspec()],
        out_specs=vspec(),
        scratch_shapes=[
            pltpu.VMEM((NDP, SEQ_DEV, 8 * HD), jnp.bfloat16),
            pltpu.VMEM((NDP * SEQ_DEV, 256), jnp.float32),
            pltpu.VMEM((NT, NDP * SEQ_DEV // NT, 256), jnp.float32),
            dma((NZ,)), dma((NZ,)), dma((NDP,)), dma((NDP,)), dma((NT,)), dma((NT,)), dma((NT,)), dma((NT,)),
        ],
        compiler_params=pltpu.CompilerParams(
            collective_id=1, has_side_effects=True, vmem_limit_bytes=VMEM_LIMIT // 2
        ),
    )(attention, out_weight)
    return new_pages.reshape(kv_pages.shape), projected


def solution(mesh):
    placed = (
        P("dp", "tensor", None),
        P("dp", "tensor", None, None, None),
        P("dp", None, None),
        P("dp"),
        P("dp", None),
        P("dp"),
        P("tensor", "dp"),
    )
    return jax.shard_map(
        body,
        mesh=mesh,
        in_specs=placed,
        out_specs=(P("dp", "tensor", None, None, None), P(None, "dp")),
        check_vma=False,
    )
```

time: 231 us -> 160 us (0.69)
  Pallas kernels: 0 us -> 147 us
  waiting for transfers between devices: 93.9 us -> 0 us
  blocking collectives: 55.6 us -> 0 us
  local copies, waits for them, and re-layouts: 37.9 us -> 11.6 us
  starting transfers between devices: 21.5 us -> 0 us
  matrix products: 16.8 us -> 0 us
  other arithmetic: 3.4 us -> 0 us
    pallas_call x0 -> x4, Pallas kernels: none -> 147 us  [the longest x1 107 us: body(): pl.pallas_call(exchange_kernel, name='exchange', out_shape=[pltpu.VMEM((S...]
    all_to_all x2 -> x0, waiting for transfers between devices: 93.9 us -> none  [the longest x1 93.9 us: body(): lax.all_to_all(outgoing, 'dp', split_axis=0, concat_axis=0, tiled=True)]
    all_to_all x2 -> x0, blocking collectives: 55.6 us -> none  [copy_for_each(): return lax.all_to_all(copies, axis, split_axis=0, concat_axis=0, tiled=True)]
    all_to_all x2 -> x0, starting transfers between devices: 21.5 us -> none  [the longest x1 12 us: body(): lax.all_to_all(slot_tags, 'dp', split_axis=0, concat_axis=0, tiled=True)]
    gather x2 -> x0, local copies, waits for them, and re-layouts: 15.9 us -> none  [the longest x1 10.3 us: body(): picked = flat_pages[move_list[0]]]
    dot_general x4 -> x0, matrix products: 14.4 us -> none  [the longest x1 10.4 us: body(): jnp.dot(hit_table.astype(jnp.bfloat16), arrived.reshape(holding_rows, -1)...]
    unnamed x12 -> x18, local copies, waits for them, and re-layouts: 16.9 us -> 11.6 us
    slice x1 -> x0, local copies, waits for them, and re-layouts: 4.03 us -> none  [body(): gathered[:, :, :, 0]]
  transfers between devices with their start and end apart: 2 -> 0, of which waited for: 1 -> 0; matrix products, arithmetic and copies ran while one was open for 12% -> 0% of each run, Pallas kernels for 0% -> 0%
where the time goes in v1:
time: 160 us
  Pallas kernels  147 us (92%)
  local copies, waits for them, and re-layouts  11.6 us (7%)
    pallas_call x1, Pallas kernels, body(): pl.pallas_call(exchange_kernel, name='exchange', out_shape=[pltpu.VMEM((S...  107 us
    pallas_call x1, Pallas kernels, body(): pl.pallas_call(project_kernel, name='project', out_shape=jax.ShapeDtypeSt...  26.8 us
    unnamed x18, local copies, waits for them, and re-layouts  11.6 us
    pallas_call x1, Pallas kernels, body(): pl.pallas_call(attend_kernel, name='attend', out_shape=[jax.ShapeDtypeStr...  7.13 us
    pallas_call x1, Pallas kernels, body(): pl.pallas_call(pack_kernel, name='pack', out_shape=[pltpu.VMEM((NDP * CAP...  5.85 us

profile of v1, /device:TPU:1, one launch (start us, length us, event | category | flops | bytes accessed | tf_op | source)
XLA Modules:
  0.0 160.0 jit_solution(4279266100826433963)
XLA Ops:
  1.3 0.7 copy.12
  2.0 0.0 copy-start
  2.0 2.6 %copy-done = bf16[88,1,2,128,128]{4,3,2,1,0:T(8,128)(2,1)S(1)} copy-done((bf16[88,1,2,128,128]{4,3,2,1,0:T(8,128)(2,1)S(1)}, bf16[88,1,2,128,128]{4,3,2,1,0:T(8,128)(2,1)}, u32[]{:S(2)}) %copy-start) | copy-done | bytes 5767192
  4.6 0.0 copy-start.1
  4.6 5.9 %pack.1 = (bf16[64,2,128,128]{3,2,1,0:T(8,128)(2,1)S(1)}, s32[32,1,128]{2,1,0:T(1,128)S(1)}) custom-call(s32[3,48]{1,0:T(4,128)S(1)} %bitcast.11, s32[1]{0:T(128)S(6)} %copy.14.count_ref, bf16[88,2,128,128]{3,2,1,0:T(8,128)(2,1)S(1)} %bitcast.8), custom_call_target="tpu_custom_call" | custom-call | tf_op jit(solution)/shard_map/pack/pallas_call | solution.py:226
  10.5 0.0 copy-start.5
  10.5 0.0 copy-start.6
  10.5 0.0 copy-start.7
  10.5 0.0 copy-done.1
  10.5 0.0 copy-start.4
  10.5 107.2 %exchange.1 = (bf16[152,2,128,128]{3,2,1,0:T(8,128)(2,1)S(1)}, s32[32,1,128]{2,1,0:T(1,128)S(1)}) custom-call(bf16[64,2,128,128]{3,2,1,0:T(8,128)(2,1)S(1)} %get-tuple-element.8.send_ref, s32[32,1,128]{2,1,0:T(1,128)S(1)} %get-tuple-element.9.tags_ref, bf16[88,2,128,128]{3,2,1,0:T(8,128)(2,1)S(1)} %bitcast.9), custom_call_target="tpu_custom_call" | custom-call | tf_op jit(solution)/shard_map/exchange/pallas_call | solution.py:235
  117.7 0.0 copy-start.2
  117.7 3.8 %copy-done.2 = bf16[152,2,128,128]{3,2,1,0:T(8,128)(2,1)} copy-done((bf16[152,2,128,128]{3,2,1,0:T(8,128)(2,1)}, bf16[152,2,128,128]{3,2,1,0:T(8,128)(2,1)S(1)}, u32[]{:S(2)}) %copy-start.2) | copy-done | bytes 9961496
  121.5 0.0 copy-done.5
  121.5 0.0 copy-done.6
  121.5 0.0 copy-done.7
  121.5 0.0 copy-start.3
  121.5 3.8 %copy-done.3 = bf16[152,2,128,128]{3,2,1,0:T(8,128)(2,1)S(1)} copy-done((bf16[152,2,128,128]{3,2,1,0:T(8,128)(2,1)S(1)}, bf16[152,2,128,128]{3,2,1,0:T(8,128)(2,1)}, u32[]{:S(2)}) %copy-start.3) | copy-done | bytes 9961496
  125.4 7.1 %attend.1 = (bf16[88,2,128,128]{3,2,1,0:T(8,128)(2,1)}, bf16[8,1024]{1,0:T(8,128)(2,1)S(1)}) custom-call(s32[32,128]{1,0:T(8,128)S(1)} %bitcast.10, s32[8,8]{1,0:T(8,128)S(1)} %copy-done.6, s32[8]{0:T(128)S(1)} %copy-done.7, bf16[8,8,128]{2,1,0:T(8,128)(2,1)S(1)} %copy-done.5, bf16[152,2,128,128]{3,2,1,0:T(8,128)(2,1)S(1)} %copy-done.3), custom_call_target="tpu_custom_call" | custom-call | tf_op jit(solution)/shard_map/attend/pallas_call | solution.py:246
  132.5 0.0 copy-done.4
  132.5 26.8 %project.1 = bf16[256,256]{1,0:T(8,128)(2,1)S(1)} custom-call(bf16[8,1024]{1,0:T(8,128)(2,1)S(1)} %get-tuple-element.13.att_ref, bf16[1024,256]{1,0:T(8,128)(2,1)S(1)} %copy-done.4), custom_call_target="tpu_custom_call" | custom-call | tf_op jit(solution)/shard_map/project/pallas_call | solution.py:258
  159.4 0.7 copy.15
Async XLA Ops:
  2.0 2.6 %copy-start = (bf16[88,1,2,128,128]{4,3,2,1,0:T(8,128)(2,1)S(1)}, bf16[88,1,2,128,128]{4,3,2,1,0:T(8,128)(2,1)}, u32[]{:S(2)}) copy-start(bf16[88,1,2,128,128]{4,3,2,1,0:T(8,128)(2,1)} %param.8) | copy-start | bytes 17301508
  4.6 5.9 %copy-start.1 = (bf16[88,1,2,128,128]{4,3,2,1,0:T(8,128)(2,1)S(1)}, bf16[88,1,2,128,128]{4,3,2,1,0:T(8,128)(2,1)}, u32[]{:S(2)}) copy-start(bf16[88,1,2,128,128]{4,3,2,1,0:T(8,128)(2,1)} %param.8) | copy-start | bytes 17301508
  10.5 111.1 %copy-start.5 = (bf16[8,8,128]{2,1,0:T(8,128)(2,1)S(1)}, bf16[8,8,128]{2,1,0:T(8,128)(2,1)}, u32[]{:S(2)}) copy-start(bf16[8,8,128]{2,1,0:T(8,128)(2,1)} %query_ref.1) | copy-start | bytes 49156
  10.5 111.1 %copy-start.6 = (s32[8,8]{1,0:T(8,128)S(1)}, s32[8,8]{1,0:T(8,128)}, u32[]{:S(2)}) copy-start(s32[8,8]{1,0:T(8,128)} %table_ref.1) | copy-start | bytes 772
  10.5 111.1 %copy-start.7 = (s32[8]{0:T(128)S(1)}, s32[8]{0:T(128)}, u32[]{:S(2)}) copy-start(s32[8]{0:T(128)} %lens_ref.1) | copy-start | bytes 100
  10.5 122.0 %copy-start.4 = (bf16[1024,256]{1,0:T(8,128)(2,1)S(1)}, bf16[1024,256]{1,0:T(8,128)(2,1)}, u32[]{:S(2)}) copy-start(bf16[1024,256]{1,0:T(8,128)(2,1)} %w_ref.1) | copy-start | bytes 1572868
  117.7 3.8 %copy-start.2 = (bf16[152,2,128,128]{3,2,1,0:T(8,128)(2,1)}, bf16[152,2,128,128]{3,2,1,0:T(8,128)(2,1)S(1)}, u32[]{:S(2)}) copy-start(bf16[152,2,128,128]{3,2,1,0:T(8,128)(2,1)S(1)} %get-tuple-element.11.comb_ref) | copy-start | bytes 29884420
  121.5 3.8 %copy-start.3 = (bf16[152,2,128,128]{3,2,1,0:T(8,128)(2,1)S(1)}, bf16[152,2,128,128]{3,2,1,0:T(8,128)(2,1)}, u32[]{:S(2)}) copy-start(bf16[152,2,128,128]{3,2,1,0:T(8,128)(2,1)} %copy-done.2) | copy-start | bytes 29884420

commit v2 on v1

v2 whole, which is shorter than its diff:
```python
import functools
import math

import jax
import jax.numpy as jnp
from jax import lax
from jax.experimental import pallas as pl
from jax.experimental.pallas import tpu as pltpu
from jax.sharding import PartitionSpec as P

HD = 128
BLOCK = 128
BLOCKS = 8
CAP = 2
SLOTS = 88
MOVES = 48
NY, NZ = 4, 8
NDP = NY * NZ
NT = 8
SEQ_DEV = 8
HEADS = 8
WINDOW = 8
NEG = -1e30
SCALE = 1.0 / math.sqrt(HD)
MESH = pl.DeviceIdType.MESH
VMEM_LIMIT = 16 * 1024 * 1024
PAGE = (2, BLOCK, HD)
SHIFTS = [(dy, dz) for dy in range(NY) for dz in range(NZ)]
f32 = jnp.float32
bf16 = jnp.bfloat16


def far(shift):
    return min(shift[0], NY - shift[0]) + min(shift[1], NZ - shift[1])


def vspec():
    return pl.BlockSpec(memory_space=pltpu.VMEM)


def sspec():
    return pl.BlockSpec(memory_space=pltpu.SMEM)


def hspec():
    return pl.BlockSpec(memory_space=pltpu.HBM)


def pack_kernel(plan_ref, count_ref, table_ref, lens_ref, kv_ref, send_ref, tags_ref, meta_ref, used, sems):
    me = lax.axis_index("dp")
    y, z = me // NZ, me % NZ
    for k in range(NDP):
        used[k] = 0
    count = count_ref[0]
    rows = lax.broadcasted_iota(jnp.int32, (NDP, 128), 0)
    cols = lax.broadcasted_iota(jnp.int32, (NDP, 128), 1)

    def step(m, tags):
        valid = m < count
        target = plan_ref[1, 0, m]
        shift = lax.rem(target // NZ - y + NY, NY) * NZ + lax.rem(target % NZ - z + NZ, NZ)
        rank = used[shift]

        @pl.when(valid)
        def _():
            used[shift] = rank + 1
            pltpu.make_async_copy(
                kv_ref.at[plan_ref[0, 0, m]], send_ref.at[shift * CAP + rank], sems.at[m]
            ).start()

        hit = (rows == shift) & (cols == rank) & valid
        return jnp.where(hit, plan_ref[2, 0, m], tags)

    tags = lax.fori_loop(0, MOVES, step, jnp.full((NDP, 128), -1, jnp.int32))
    tags_ref[...] = tags.reshape(NDP, 1, 128)
    lane = lax.broadcasted_iota(jnp.int32, (1, 128), 1)
    meta = jnp.full((1, 128), -2, jnp.int32)
    for s in range(SEQ_DEV):
        for b in range(BLOCKS):
            meta = jnp.where(lane == s * BLOCKS + b, table_ref[s, b], meta)
        meta = jnp.where(lane == SEQ_DEV * BLOCKS + s, lens_ref[s], meta)
    meta_ref[0] = meta

    def drain(m, carry):
        @pl.when(m < count)
        def _():
            pltpu.make_async_copy(kv_ref.at[0], send_ref.at[0], sems.at[m]).wait()

        return carry

    lax.fori_loop(0, MOVES, drain, 0)


def step_kernel(
    table_ref, lens_ref, send_ref, tags_ref, meta_ref, query_ref, w_ref, kv_ref,
    local_ref, recv_ref, code_ref, out_ref,
    got, metas, qall, src_seq, src_end, arr_seq, part, lse, apart, alse, wide, mixed, att, gath, proj, red,
    load_sem, page_send, page_recv, tag_sem, meta_sem, part_sem, lse_sem,
    qz_send, qz_recv, qy_send, qy_recv, z_send, z_recv, y_send, y_recv, r_send, r_recv, o_send, o_recv,
):
    me = lax.axis_index("dp")
    t = lax.axis_index("tensor")
    y, z = me // NZ, me % NZ
    zs = [lax.rem(z + d, NZ) for d in range(NZ)]
    ys = [lax.rem(y + d, NY) for d in range(NY)]
    ts = [lax.rem(t + d, NT) for d in range(NT)]
    load = pltpu.make_async_copy(kv_ref, local_ref, load_sem)
    load.start()
    bar = pltpu.get_barrier_semaphore()
    order = sorted([s for s in SHIFTS if s != (0, 0)], key=lambda s: -far(s))
    peers = [(ys[dy] * NZ + zs[dz], t) for dy, dz in order] + [(me, ts[d]) for d in range(1, NT)]
    for peer in peers:
        pl.semaphore_signal(bar, inc=1, device_id=peer, device_id_type=MESH)
    pl.semaphore_wait(bar, len(peers))

    def remote(src, dst, send, recv, device):
        copy = pltpu.make_async_remote_copy(
            src_ref=src, dst_ref=dst, send_sem=send, recv_sem=recv, device_id=device, device_id_type=MESH
        )
        copy.start()
        return copy

    def to(shift):
        return (ys[shift[0]] * NZ + zs[shift[1]], t)

    def at(shift):
        return shift[0] * NZ + shift[1]

    pages = []
    pending = [(c, s) for c in range(CAP) for s in order]

    def pump(n):
        for _ in range(n):
            i = len(pages)
            if i >= len(pending):
                return
            if i >= WINDOW:
                pages[i - WINDOW].wait_send()
            c, s = pending[i]
            row = at(s) * CAP + c
            pages.append(
                remote(send_ref.at[row], recv_ref.at[row], page_send.at[i % WINDOW], page_recv.at[0], to(s))
            )

    z_order = sorted(range(1, NZ), key=lambda d: -min(d, NZ - d))
    z_near = sorted(range(1, NZ), key=lambda d: min(d, NZ - d))

    def gather_start(own_ref, buf, zsend, zrecv, ysend, yrecv):
        along_z = {d: remote(own_ref, buf.at[me], zsend.at[d], zrecv.at[d], (y * NZ + zs[d], t)) for d in z_order}
        along_y = [
            remote(own_ref, buf.at[me], ysend.at[d], yrecv.at[d], (ys[d] * NZ + z, t)) for d in (2, 1, 3)
        ]
        buf[me] = own_ref[...]
        return along_z, along_y

    def gather_forward(along_z, along_y, buf, ysend, yrecv, pumps):
        for e in z_near:
            along_z[e].wait_recv()
            held = y * NZ + lax.rem(z - e + NZ, NZ)
            for d in (2, 1, 3):
                n = e * NY + d
                along_y.append(
                    remote(buf.at[held], buf.at[held], ysend.at[n], yrecv.at[n], (ys[d] * NZ + z, t))
                )
            pump(pumps)

    q_z, q_y = gather_start(query_ref, qall, qz_send, qz_recv, qy_send, qy_recv)
    small = []
    for s in order:
        back = ((NY - s[0]) % NY, (NZ - s[1]) % NZ)
        small.append(remote(tags_ref.at[at(s)], got.at[at(s)], tag_sem.at[0], tag_sem.at[1], to(s)))
        small.append(remote(meta_ref.at[0], metas.at[at(back)], meta_sem.at[0], meta_sem.at[1], to(s)))
    got[0] = tags_ref[0]
    metas[0] = meta_ref[0]
    pump(WINDOW)
    recv_ref[0:CAP] = send_ref[0:CAP]
    gather_forward(q_z, q_y, qall, qy_send, qy_recv, 1)

    def all_of(buf, sems):
        return pltpu.make_async_remote_copy(
            src_ref=buf.at[pl.ds(1, NDP - 1)],
            dst_ref=buf.at[pl.ds(1, NDP - 1)],
            send_sem=sems.at[0],
            recv_sem=sems.at[1],
            device_id=(me, ts[1]),
            device_id_type=MESH,
        )

    all_of(got, tag_sem).wait_recv()
    all_of(metas, meta_sem).wait_recv()
    lane = lax.broadcasted_iota(jnp.int32, (NDP, 128), 1)
    lane_f = lane.astype(f32)
    first = lane < SEQ_DEV * BLOCKS
    seq_f = (lane // BLOCKS).astype(f32)
    block_f = (lane % BLOCKS).astype(f32)
    device_f = lax.broadcasted_iota(jnp.int32, (NDP, 128), 0).astype(f32)
    mine = metas[0]
    moved = jnp.zeros((1, 128), f32)
    code = jnp.zeros((1, 128), f32)
    sent_tags = tags_ref[...].reshape(NDP, 128)
    got_tags = got[...].reshape(NDP, 128)
    tables = metas[...].reshape(NDP, 128)

    def spread(column):
        return jnp.broadcast_to(column, (NDP, 128)).reshape(NDP, 1, 128)

    for c in range(CAP):
        tag = sent_tags[:, c : c + 1]
        hit = (tables == tag) & first & (tag >= 0)
        found = jnp.sum(jnp.where(hit, 1.0, 0.0), axis=1, keepdims=True)
        seq = jnp.sum(jnp.where(hit, seq_f, 0.0), axis=1, keepdims=True)
        block = jnp.sum(jnp.where(hit, block_f, 0.0), axis=1, keepdims=True)
        ends = jnp.sum(
            jnp.where(lane_f == seq + SEQ_DEV * BLOCKS, tables.astype(f32), 0.0), axis=1, keepdims=True
        )
        src_seq[c] = spread(jnp.where(found > 0, seq, -1.0))
        src_end[c] = spread(ends - block * BLOCK)
        tag = got_tags[:, c : c + 1]
        hit = (mine == tag) & first & (tag >= 0)
        found = jnp.sum(jnp.where(hit, 1.0, 0.0), axis=1, keepdims=True)
        seq = jnp.sum(jnp.where(hit, seq_f, 0.0), axis=1, keepdims=True)
        arr_seq[c] = spread(jnp.where(found > 0, seq, -1.0))
        moved = jnp.maximum(moved, jnp.max(jnp.where(hit, 1.0, 0.0), axis=0, keepdims=True))
        code = code + jnp.sum(jnp.where(lane == tag, device_f * CAP + (c + 1), 0.0), axis=0, keepdims=True)
    code_ref[...] = code.astype(jnp.int32)
    pump(2)

    load.wait()
    position = lax.broadcasted_iota(jnp.int32, (HEADS, BLOCKS * BLOCK), 1)
    kept_o = []
    kept_lse = []
    for s in range(SEQ_DEV):
        index = [table_ref[s, b] for b in range(BLOCKS)]
        keys = jnp.concatenate([local_ref[i, 0] for i in index], axis=0)
        scores = lax.dot_general(
            query_ref[s * HEADS : (s + 1) * HEADS, :], keys, (((1,), (1,)), ((), ())), preferred_element_type=f32
        ) * SCALE
        gone = jnp.concatenate(
            [jnp.broadcast_to(moved[:, s * BLOCKS + b : s * BLOCKS + b + 1], (1, BLOCK)) for b in range(BLOCKS)], axis=1
        )
        scores = jnp.where((position < lens_ref[s]) & (gone == 0), scores, NEG)
        largest = jnp.max(scores, axis=1, keepdims=True)
        expo = jnp.exp(scores - largest)
        total = jnp.sum(expo, axis=1, keepdims=True)
        values = jnp.concatenate([local_ref[i, 1] for i in index], axis=0)
        mixed[s * HEADS : (s + 1) * HEADS, :] = (
            jnp.dot(expo.astype(bf16), values, preferred_element_type=f32) / total
        )
        wide[s] = jnp.broadcast_to(largest + jnp.log(total), (HEADS, 128))
        if s % 2:
            pump(1)

    for copy in q_y:
        copy.wait_recv()
    lane8 = lax.broadcasted_iota(jnp.int32, (HEADS, 128), 1)
    row8 = lax.broadcasted_iota(jnp.int32, (HEADS, 128), 0)
    lane8_f = lane8.astype(f32)

    def rows8(ref, c, k):
        return jnp.broadcast_to(ref[c, k], (HEADS, 128))

    def partial(k, carry):
        dy, dz = k // NZ, lax.rem(k, NZ)
        owner = lax.rem(y + dy, NY) * NZ + lax.rem(z + dz, NZ)
        asked = qall[owner]
        keys = jnp.concatenate([send_ref[k * CAP + c, 0] for c in range(CAP)], axis=0)
        every = lax.dot_general(asked, keys, (((1,), (1,)), ((), ())), preferred_element_type=f32) * SCALE
        row = jnp.zeros((1, 128), f32)
        for c in range(CAP):
            seq = rows8(src_seq, c, k)
            scores = jnp.full((HEADS, BLOCK), NEG, f32)
            for s in range(SEQ_DEV):
                scores = jnp.where(
                    seq == s, every[s * HEADS : (s + 1) * HEADS, c * BLOCK : (c + 1) * BLOCK], scores
                )
            scores = jnp.where(lane8_f < rows8(src_end, c, k), scores, NEG)
            largest = jnp.max(scores, axis=1, keepdims=True)
            expo = jnp.exp(scores - largest)
            total = jnp.sum(expo, axis=1, keepdims=True)
            o = jnp.dot(expo.astype(bf16), send_ref[k * CAP + c, 1], preferred_element_type=f32) / total
            part[k, c] = jnp.where(seq >= 0, o, 0.0).astype(bf16)
            weight = jnp.where(seq >= 0, largest + jnp.log(total), NEG)
            row = row + jnp.sum(jnp.where(lane8 == row8 + c * HEADS, weight, 0.0), axis=0, keepdims=True)
        lse[k] = row
        return carry

    for g in range(4):
        lax.fori_loop(g * NZ, (g + 1) * NZ, partial, 0)
        for dz in range(NZ):
            if (g, dz) != (0, 0):
                k = at((g, dz))
                small.append(remote(part.at[k], apart.at[k], part_sem.at[0], part_sem.at[1], to((g, dz))))
                small.append(remote(lse.at[k], alse.at[k], lse_sem.at[0], lse_sem.at[1], to((g, dz))))
        pump(2)
    apart[0] = part[0]
    alse[0] = lse[0]
    pump(3)
    all_of(apart, part_sem).wait_recv()
    all_of(alse, lse_sem).wait_recv()

    def widen(k, tops):
        tops = list(tops)
        for c in range(CAP):
            column = jnp.sum(
                jnp.where(lane8 == row8 + c * HEADS, jnp.broadcast_to(alse[k], (HEADS, 128)), 0.0),
                axis=1,
                keepdims=True,
            )
            full = jnp.broadcast_to(column, (HEADS, 128))
            wide[SEQ_DEV + k * CAP + c] = full
            seq = rows8(arr_seq, c, k)
            for s in range(SEQ_DEV):
                tops[s] = jnp.where(seq == s, jnp.maximum(tops[s], full), tops[s])
        return tuple(tops)

    tops = lax.fori_loop(0, NDP, widen, tuple(wide[s] for s in range(SEQ_DEV)))
    start = []
    for s in range(SEQ_DEV):
        w = jnp.exp(wide[s] - tops[s])
        start.append((w, w * mixed[s * HEADS : (s + 1) * HEADS, :]))

    def merge(k, sums):
        dens, nums = list(sums[0]), list(sums[1])
        for c in range(CAP):
            seq = rows8(arr_seq, c, k)
            top = jnp.zeros((HEADS, 128), f32)
            for s in range(SEQ_DEV):
                top = jnp.where(seq == s, tops[s], top)
            w = jnp.exp(wide[SEQ_DEV + k * CAP + c] - top)
            o = w * apart[k, c].astype(f32)
            for s in range(SEQ_DEV):
                dens[s] = jnp.where(seq == s, dens[s] + w, dens[s])
                nums[s] = jnp.where(seq == s, nums[s] + o, nums[s])
        return tuple(dens), tuple(nums)

    dens, nums = lax.fori_loop(
        0, NDP, merge, (tuple(a for a, _ in start), tuple(b for _, b in start))
    )
    for s in range(SEQ_DEV):
        mixed[s * HEADS : (s + 1) * HEADS, :] = nums[s] / dens[s]
    att[...] = jnp.concatenate(
        [mixed[pl.ds(h, SEQ_DEV, stride=HEADS), :] for h in range(HEADS)], axis=1
    ).astype(bf16)

    along_z, along_y = gather_start(att, gath, z_send, z_recv, y_send, y_recv)
    pump(4)
    gather_forward(along_z, along_y, gath, y_send, y_recv, 1)
    pump(2)
    for copy in along_y:
        copy.wait_recv()
    rows = gath[...].reshape(NDP * SEQ_DEV, HEADS * HD)
    proj[...] = jnp.dot(rows, w_ref[...], preferred_element_type=f32)
    chunk = NDP * SEQ_DEV // NT
    t_order = (4, 5, 3, 2, 6, 1, 7)

    def rows_of(i):
        return pl.ds(pl.multiple_of(i * chunk, chunk), chunk)

    sums = [remote(proj.at[rows_of(ts[d])], red.at[d], r_send.at[d], r_recv.at[d], (me, ts[d])) for d in t_order]
    pump(2)
    total = proj[rows_of(t), :]
    for copy in sums:
        copy.wait_recv()
    for d in range(1, NT):
        total = total + red[d]
    out_ref[rows_of(t), :] = total.astype(bf16)
    outs = [
        remote(out_ref.at[rows_of(t)], out_ref.at[rows_of(t)], o_send.at[d], o_recv.at[d], (me, ts[d])) for d in t_order
    ]
    pump(len(pending))
    for copy in outs:
        copy.wait_recv()
    for copy in pages[-WINDOW:]:
        copy.wait_send()
    for copy in list(q_z.values()) + q_y + list(along_z.values()) + along_y + sums + outs:
        copy.wait_send()
    all_of(got, tag_sem).wait_send()
    all_of(metas, meta_sem).wait_send()
    all_of(part, part_sem).wait_send()
    all_of(lse, lse_sem).wait_send()
    moved_pages = recv_ref.at[pl.ds(CAP, (NDP - 1) * CAP)]
    pltpu.make_async_remote_copy(
        src_ref=moved_pages, dst_ref=moved_pages, send_sem=page_send.at[0], recv_sem=page_recv.at[0],
        device_id=(me, ts[1]), device_id_type=MESH,
    ).wait_recv()


def place_kernel(code_ref, local_ref, recv_ref, proj_ref, new_ref, out_ref, sems, out_sem):
    result = pltpu.make_async_copy(proj_ref, out_ref, out_sem)
    result.start()

    def put(s, carry):
        code = code_ref[0, s]

        @pl.when(code == 0)
        def _():
            pltpu.make_async_copy(local_ref.at[s], new_ref.at[s], sems.at[s]).start()

        @pl.when(code > 0)
        def _():
            pltpu.make_async_copy(recv_ref.at[code - 1], new_ref.at[s], sems.at[s]).start()

        return carry

    lax.fori_loop(0, SLOTS, put, 0)

    def drain(s, carry):
        pltpu.make_async_copy(local_ref.at[0], new_ref.at[0], sems.at[s]).wait()
        return carry

    lax.fori_loop(0, SLOTS, drain, 0)
    result.wait()


def body(query, kv_pages, move_plan, move_count, block_table, seq_lens, out_weight):
    kv = kv_pages.reshape(SLOTS, *PAGE)
    dma = pltpu.SemaphoreType.DMA
    i32 = jnp.int32
    columns = out_weight.shape[1]
    seqs = NDP * SEQ_DEV
    send, tags, meta = pl.pallas_call(
        pack_kernel,
        name="pack",
        out_shape=[pltpu.VMEM((NDP * CAP, *PAGE), bf16), pltpu.VMEM((NDP, 1, 128), i32), pltpu.VMEM((1, 1, 128), i32)],
        in_specs=[sspec(), sspec(), sspec(), sspec(), hspec()],
        out_specs=[vspec()] * 3,
        scratch_shapes=[pltpu.SMEM((NDP,), i32), dma((MOVES,))],
        compiler_params=pltpu.CompilerParams(vmem_limit_bytes=VMEM_LIMIT),
    )(jnp.transpose(move_plan, (1, 0, 2)), move_count, block_table, seq_lens, kv)
    local, recv, code, projected = pl.pallas_call(
        step_kernel,
        name="step",
        out_shape=[
            pltpu.VMEM((SLOTS, *PAGE), bf16),
            pltpu.VMEM((NDP * CAP, *PAGE), bf16),
            pltpu.VMEM((1, 128), i32),
            pltpu.VMEM((seqs, columns), bf16),
        ],
        in_specs=[sspec(), sspec(), vspec(), vspec(), vspec(), vspec(), vspec(), hspec()],
        out_specs=[vspec()] * 4,
        scratch_shapes=[
            pltpu.VMEM((NDP, 1, 128), i32),
            pltpu.VMEM((NDP, 1, 128), i32),
            pltpu.VMEM((NDP, SEQ_DEV * HEADS, HD), bf16),
            pltpu.VMEM((CAP, NDP, 1, 128), f32),
            pltpu.VMEM((CAP, NDP, 1, 128), f32),
            pltpu.VMEM((CAP, NDP, 1, 128), f32),
            pltpu.VMEM((NDP, CAP, HEADS, HD), bf16),
            pltpu.VMEM((NDP, 1, 128), f32),
            pltpu.VMEM((NDP, CAP, HEADS, HD), bf16),
            pltpu.VMEM((NDP, 1, 128), f32),
            pltpu.VMEM((SEQ_DEV + NDP * CAP, HEADS, 128), f32),
            pltpu.VMEM((SEQ_DEV * HEADS, HD), f32),
            pltpu.VMEM((SEQ_DEV, HEADS * HD), bf16),
            pltpu.VMEM((NDP, SEQ_DEV, HEADS * HD), bf16),
            pltpu.VMEM((seqs, columns), f32),
            pltpu.VMEM((NT, seqs // NT, columns), f32),
            dma(()), dma((WINDOW,)), dma((1,)), dma((2,)), dma((2,)), dma((2,)), dma((2,)),
            dma((NZ,)), dma((NZ,)), dma((NDP,)), dma((NDP,)),
            dma((NZ,)), dma((NZ,)), dma((NDP,)), dma((NDP,)),
            dma((NT,)), dma((NT,)), dma((NT,)), dma((NT,)),
        ],
        compiler_params=pltpu.CompilerParams(
            collective_id=0, has_side_effects=True, vmem_limit_bytes=VMEM_LIMIT
        ),
    )(block_table, seq_lens, send, tags, meta, query.reshape(SEQ_DEV * HEADS, HD), out_weight, kv)
    new_pages, projected = pl.pallas_call(
        place_kernel,
        name="place",
        out_shape=[
            jax.ShapeDtypeStruct((SLOTS, *PAGE), bf16),
            jax.ShapeDtypeStruct((seqs, columns), bf16),
        ],
        in_specs=[sspec(), vspec(), vspec(), vspec()],
        out_specs=[hspec(), hspec()],
        scratch_shapes=[dma((SLOTS,)), dma(())],
        compiler_params=pltpu.CompilerParams(vmem_limit_bytes=VMEM_LIMIT),
    )(code, local, recv, projected)
    return new_pages.reshape(kv_pages.shape), projected


def solution(mesh):
    placed = (
        P("dp", "tensor", None),
        P("dp", "tensor", None, None, None),
        P("dp", None, None),
        P("dp"),
        P("dp", None),
        P("dp"),
        P("tensor", "dp"),
    )
    return jax.shard_map(
        body,
        mesh=mesh,
        in_specs=placed,
        out_specs=(P("dp", "tensor", None, None, None), P(None, "dp")),
        check_vma=False,
    )
```

time: 160 us -> 135 us (0.84)
  Pallas kernels: 147 us -> 127 us
  local copies, waits for them, and re-layouts: 11.6 us -> 6.41 us
    pallas_call x3 -> x2, Pallas kernels: 141 us -> 121 us  [the longest x1 118 us: body(): pl.pallas_call(step_kernel, name='step', out_shape=[pltpu.VMEM((SLOTS, *P...]
    unnamed x18 -> x16, local copies, waits for them, and re-layouts: 11.6 us -> 6.41 us
where the time goes in v2:
time: 135 us
  Pallas kernels  127 us (94%)
  local copies, waits for them, and re-layouts  6.41 us (5%)
  between operations  1.35 us (1%)
    pallas_call x1, Pallas kernels, body(): pl.pallas_call(step_kernel, name='step', out_shape=[pltpu.VMEM((SLOTS, *P...  118 us
    unnamed x16, local copies, waits for them, and re-layouts  6.41 us
    pallas_call x1, Pallas kernels, body(): pl.pallas_call(pack_kernel, name='pack', out_shape=[pltpu.VMEM((NDP * CAP...  5.86 us
    pallas_call x1, Pallas kernels, body(): pl.pallas_call(place_kernel, name='place', out_shape=[jax.ShapeDtypeStruc...  3.8 us

profile of v2, /device:TPU:1, one launch (start us, length us, event | category | flops | bytes accessed | tf_op | source)
XLA Modules:
  0.0 135.0 jit_solution(5816276047600926555)
XLA Ops:
  0.6 0.0 copy-start.4
  1.3 0.0 copy-start
  1.3 2.6 %copy-done = bf16[88,1,2,128,128]{4,3,2,1,0:T(8,128)(2,1)S(1)} copy-done((bf16[88,1,2,128,128]{4,3,2,1,0:T(8,128)(2,1)S(1)}, bf16[88,1,2,128,128]{4,3,2,1,0:T(8,128)(2,1)}, u32[]{:S(2)}) %copy-start) | copy-done | bytes 5767192
  3.9 0.0 copy-start.3
  3.9 0.7 copy-done.3
  4.6 0.0 copy-start.6
  4.6 0.7 copy-done.6
  5.3 0.0 copy-start.7
  5.3 0.7 copy-done.7
  6.0 0.0 copy-start.1
  6.0 5.9 %pack.1 = (bf16[64,2,128,128]{3,2,1,0:T(8,128)(2,1)S(1)}, s32[32,1,128]{2,1,0:T(1,128)S(1)}, s32[1,1,128]{2,1,0:T(1,128)S(1)}) custom-call(s32[3,1,48]{2,1,0:T(1,128)S(1)} %bitcast.9, s32[1]{0:T(128)S(6)} %copy.10.count_ref, s32[8,8]{1,0:T(8,128)S(1)} %copy-done.3, s32[8]{0:T(128)S(1)} %copy-done.6, bf16[88,2,128,128]{3,2,1,0:T(8,128)(2,1)S(1)} %bitcast.6), custom_call_target="tpu_custom_call" | custom-call | tf_op jit(solution)/shard_map/pack/pallas_call | solution.py:421
  11.8 0.0 copy-done.4
  11.8 0.0 copy-done.1
  11.9 0.0 copy-start.2
  11.9 1.0 copy-done.2
  12.9 0.0 copy-start.5
  12.9 0.7 copy-done.5
  13.6 117.5 %step.1 = (bf16[88,2,128,128]{3,2,1,0:T(8,128)(2,1)S(1)}, bf16[64,2,128,128]{3,2,1,0:T(8,128)(2,1)S(1)}, s32[1,128]{1,0:T(1,128)S(1)}, bf16[256,256]{1,0:T(8,128)(2,1)S(1)}) custom-call(s32[8,8]{1,0:T(8,128)S(1)} %copy-done.4, s32[8]{0:T(128)S(1)} %copy-done.6, bf16[64,2,128,128]{3,2,1,0:T(8,128)(2,1)S(1)} %get-tuple-element.11.send_ref, ...), custom_call_target="tpu_custom_call" | custom-call | tf_op jit(solution)/shard_map/step/pallas_call | solution.py:430
  131.2 3.8 %place.1 = (bf16[88,2,128,128]{3,2,1,0:T(8,128)(2,1)}, bf16[256,256]{1,0:T(8,128)(2,1)}) custom-call(s32[1,128]{1,0:T(1,128)S(1)} %get-tuple-element.14.code_ref, bf16[88,2,128,128]{3,2,1,0:T(8,128)(2,1)S(1)} %get-tuple-element.15.local_ref, bf16[64,2,128,128]{3,2,1,0:T(8,128)(2,1)S(1)} %get-tuple-element.16.recv_ref, ...), custom_call_target="tpu_custom_call" | custom-call | tf_op jit(solution)/shard_map/place/pallas_call | solution.py:467
Async XLA Ops:
  0.6 11.2 %copy-start.4 = (s32[8,8]{1,0:T(8,128)S(1)}, s32[8,8]{1,0:T(8,128)}, u32[]{:S(2)}) copy-start(s32[8,8]{1,0:T(8,128)} %table_ref.3) | copy-start | bytes 772
  1.3 2.6 %copy-start = (bf16[88,1,2,128,128]{4,3,2,1,0:T(8,128)(2,1)S(1)}, bf16[88,1,2,128,128]{4,3,2,1,0:T(8,128)(2,1)}, u32[]{:S(2)}) copy-start(bf16[88,1,2,128,128]{4,3,2,1,0:T(8,128)(2,1)} %param.8) | copy-start | bytes 17301508
  3.9 0.7 copy-start.3
  4.6 0.7 copy-start.6
  5.3 0.7 copy-start.7
  6.0 5.9 %copy-start.1 = (bf16[88,1,2,128,128]{4,3,2,1,0:T(8,128)(2,1)S(1)}, bf16[88,1,2,128,128]{4,3,2,1,0:T(8,128)(2,1)}, u32[]{:S(2)}) copy-start(bf16[88,1,2,128,128]{4,3,2,1,0:T(8,128)(2,1)} %param.8) | copy-start | bytes 17301508
  11.9 1.0 copy-start.2
  12.9 0.7 copy-start.5

commit v3 on v2

--- a/solution.py
+++ b/solution.py
@@ -19,11 +19,11 @@
 NT = 8
 SEQ_DEV = 8
 HEADS = 8
-WINDOW = 8
+WINDOW = 16
 NEG = -1e30
 SCALE = 1.0 / math.sqrt(HD)
 MESH = pl.DeviceIdType.MESH
-VMEM_LIMIT = 16 * 1024 * 1024
+VMEM_LIMIT = 24 * 1024 * 1024
 PAGE = (2, BLOCK, HD)
 SHIFTS = [(dy, dz) for dy in range(NY) for dz in range(NZ)]
 f32 = jnp.float32
@@ -46,56 +46,11 @@
     return pl.BlockSpec(memory_space=pltpu.HBM)
 
 
-def pack_kernel(plan_ref, count_ref, table_ref, lens_ref, kv_ref, send_ref, tags_ref, meta_ref, used, sems):
-    me = lax.axis_index("dp")
-    y, z = me // NZ, me % NZ
-    for k in range(NDP):
-        used[k] = 0
-    count = count_ref[0]
-    rows = lax.broadcasted_iota(jnp.int32, (NDP, 128), 0)
-    cols = lax.broadcasted_iota(jnp.int32, (NDP, 128), 1)
-
-    def step(m, tags):
-        valid = m < count
-        target = plan_ref[1, 0, m]
-        shift = lax.rem(target // NZ - y + NY, NY) * NZ + lax.rem(target % NZ - z + NZ, NZ)
-        rank = used[shift]
-
-        @pl.when(valid)
-        def _():
-            used[shift] = rank + 1
-            pltpu.make_async_copy(
-                kv_ref.at[plan_ref[0, 0, m]], send_ref.at[shift * CAP + rank], sems.at[m]
-            ).start()
-
-        hit = (rows == shift) & (cols == rank) & valid
-        return jnp.where(hit, plan_ref[2, 0, m], tags)
-
-    tags = lax.fori_loop(0, MOVES, step, jnp.full((NDP, 128), -1, jnp.int32))
-    tags_ref[...] = tags.reshape(NDP, 1, 128)
-    lane = lax.broadcasted_iota(jnp.int32, (1, 128), 1)
-    meta = jnp.full((1, 128), -2, jnp.int32)
-    for s in range(SEQ_DEV):
-        for b in range(BLOCKS):
-            meta = jnp.where(lane == s * BLOCKS + b, table_ref[s, b], meta)
-        meta = jnp.where(lane == SEQ_DEV * BLOCKS + s, lens_ref[s], meta)
-    meta_ref[0] = meta
-
-    def drain(m, carry):
-        @pl.when(m < count)
-        def _():
-            pltpu.make_async_copy(kv_ref.at[0], send_ref.at[0], sems.at[m]).wait()
-
-        return carry
-
-    lax.fori_loop(0, MOVES, drain, 0)
-
-
 def step_kernel(
-    table_ref, lens_ref, send_ref, tags_ref, meta_ref, query_ref, w_ref, kv_ref,
-    local_ref, recv_ref, code_ref, out_ref,
-    got, metas, qall, src_seq, src_end, arr_seq, part, lse, apart, alse, wide, mixed, att, gath, proj, red,
-    load_sem, page_send, page_recv, tag_sem, meta_sem, part_sem, lse_sem,
+    count_ref, plan_hbm, table_hbm, lens_hbm, query_hbm, w_hbm, kv_ref,
+    comb_ref, code_ref, out_ref,
+    plan_ref, table_ref, lens_ref, query_ref, w_ref, local_ref, send_ref, tags_ref, meta_ref, got, metas, qall, src_seq, src_end, arr_seq, part, lse, apart, alse, wide, mixed, att, gath, proj, red,
+    in_sems, load_sem, page_send, page_recv, tag_sem, meta_sem, part_sem, lse_sem,
     qz_send, qz_recv, qy_send, qy_recv, z_send, z_recv, y_send, y_recv, r_send, r_recv, o_send, o_recv,
 ):
     me = lax.axis_index("dp")
@@ -104,13 +59,64 @@
     zs = [lax.rem(z + d, NZ) for d in range(NZ)]
     ys = [lax.rem(y + d, NY) for d in range(NY)]
     ts = [lax.rem(t + d, NT) for d in range(NT)]
-    load = pltpu.make_async_copy(kv_ref, local_ref, load_sem)
-    load.start()
+    fetch = [
+        pltpu.make_async_copy(a, b, in_sems.at[i])
+        for i, (a, b) in enumerate(
+            [(plan_hbm, plan_ref), (query_hbm, query_ref), (table_hbm, table_ref), (lens_hbm, lens_ref), (w_hbm, w_ref)]
+        )
+    ]
+    load = pltpu.make_async_copy(kv_ref, local_ref, load_sem.at[0])
+    keep = pltpu.make_async_copy(kv_ref, comb_ref.at[pl.ds(0, SLOTS)], load_sem.at[1])
+    for copy in fetch + [load, keep]:
+        copy.start()
     bar = pltpu.get_barrier_semaphore()
     order = sorted([s for s in SHIFTS if s != (0, 0)], key=lambda s: -far(s))
     peers = [(ys[dy] * NZ + zs[dz], t) for dy, dz in order] + [(me, ts[d]) for d in range(1, NT)]
     for peer in peers:
         pl.semaphore_signal(bar, inc=1, device_id=peer, device_id_type=MESH)
+
+    i32 = jnp.int32
+    for copy in fetch[:4]:
+        copy.wait()
+
+    def iota(shape, axis):
+        return lax.broadcasted_iota(i32, shape, axis)
+
+    plan = [jnp.broadcast_to(plan_ref[r], (MOVES, MOVES)) for r in range(3)]
+    down, across = iota((MOVES, MOVES), 0), iota((MOVES, MOVES), 1)
+    target = jnp.sum(jnp.where(down == across, plan[1], 0), axis=1, keepdims=True)
+    before = (target == plan[1]) & (down < across) & (down < count_ref[0])
+    rank = jnp.sum(jnp.where(before, 1, 0), axis=0, keepdims=True)
+    goes = plan_ref[1]
+    shift = (((goes >> 3) - y) & (NY - 1)) * NZ + ((goes - z) & (NZ - 1))
+    row = jnp.where(iota((1, MOVES), 1) < count_ref[0], shift * CAP + rank, -1)
+    lane = iota((NDP, 128), 1)
+    tags = jnp.full((NDP, 128), -1, i32)
+    source = []
+    for c in range(CAP):
+        hit = jnp.broadcast_to(row, (NDP, MOVES)) == iota((NDP, MOVES), 0) * CAP + c
+        source.append(
+            jnp.sum(jnp.where(hit, jnp.broadcast_to(plan_ref[0], (NDP, MOVES)), 0), axis=1, keepdims=True)
+        )
+        slot = jnp.sum(jnp.where(hit, jnp.broadcast_to(plan_ref[2], (NDP, MOVES)) + 1, 0), axis=1, keepdims=True) - 1
+        tags = jnp.where(lane == c, slot, tags)
+    tags_ref[...] = tags.reshape(NDP, 1, 128)
+    lane1 = iota((1, 128), 1)
+    meta = jnp.full((1, 128), -2, i32)
+    for s in range(SEQ_DEV):
+        for b in range(BLOCKS):
+            meta = jnp.where(lane1 == s * BLOCKS + b, table_ref[s, b], meta)
+        meta = jnp.where(lane1 == SEQ_DEV * BLOCKS + s, lens_ref[s], meta)
+    meta_ref[0] = meta
+    load.wait()
+
+    def take(c, k):
+        send_ref[k * CAP + c] = local_ref[source[c][k, 0]]
+
+    for c, (dy, dz) in [(c, s) for c in range(CAP) for s in order]:
+        take(c, dy * NZ + dz)
+    for c in range(CAP):
+        take(c, 0)
     pl.semaphore_wait(bar, len(peers))
 
     def remote(src, dst, send, recv, device):
@@ -139,7 +145,7 @@
             c, s = pending[i]
             row = at(s) * CAP + c
             pages.append(
-                remote(send_ref.at[row], recv_ref.at[row], page_send.at[i % WINDOW], page_recv.at[0], to(s))
+                remote(send_ref.at[row], comb_ref.at[SLOTS + row], page_send.at[i % WINDOW], page_recv.at[0], to(s))
             )
 
     z_order = sorted(range(1, NZ), key=lambda d: -min(d, NZ - d))
@@ -173,7 +179,7 @@
     got[0] = tags_ref[0]
     metas[0] = meta_ref[0]
     pump(WINDOW)
-    recv_ref[0:CAP] = send_ref[0:CAP]
+    comb_ref[SLOTS : SLOTS + CAP] = send_ref[0:CAP]
     gather_forward(q_z, q_y, qall, qy_send, qy_recv, 1)
 
     def all_of(buf, sems):
@@ -188,7 +194,6 @@
 
     all_of(got, tag_sem).wait_recv()
     all_of(metas, meta_sem).wait_recv()
-    lane = lax.broadcasted_iota(jnp.int32, (NDP, 128), 1)
     lane_f = lane.astype(f32)
     first = lane < SEQ_DEV * BLOCKS
     seq_f = (lane // BLOCKS).astype(f32)
@@ -196,7 +201,7 @@
     device_f = lax.broadcasted_iota(jnp.int32, (NDP, 128), 0).astype(f32)
     mine = metas[0]
     moved = jnp.zeros((1, 128), f32)
-    code = jnp.zeros((1, 128), f32)
+    code = lane1.astype(f32)
     sent_tags = tags_ref[...].reshape(NDP, 128)
     got_tags = got[...].reshape(NDP, 128)
     tables = metas[...].reshape(NDP, 128)
@@ -221,11 +226,13 @@
         seq = jnp.sum(jnp.where(hit, seq_f, 0.0), axis=1, keepdims=True)
         arr_seq[c] = spread(jnp.where(found > 0, seq, -1.0))
         moved = jnp.maximum(moved, jnp.max(jnp.where(hit, 1.0, 0.0), axis=0, keepdims=True))
-        code = code + jnp.sum(jnp.where(lane == tag, device_f * CAP + (c + 1), 0.0), axis=0, keepdims=True)
+        code = code + jnp.sum(
+            jnp.where(lane == tag, device_f * CAP + (SLOTS + c) - lane_f, 0.0), axis=0, keepdims=True
+        )
     code_ref[...] = code.astype(jnp.int32)
     pump(2)
 
-    load.wait()
+    keep.wait()
     position = lax.broadcasted_iota(jnp.int32, (HEADS, BLOCKS * BLOCK), 1)
     kept_o = []
     kept_lse = []
@@ -348,6 +355,7 @@
     pump(2)
     for copy in along_y:
         copy.wait_recv()
+    fetch[4].wait()
     rows = gath[...].reshape(NDP * SEQ_DEV, HEADS * HD)
     proj[...] = jnp.dot(rows, w_ref[...], preferred_element_type=f32)
     chunk = NDP * SEQ_DEV // NT
@@ -378,67 +386,55 @@
     all_of(metas, meta_sem).wait_send()
     all_of(part, part_sem).wait_send()
     all_of(lse, lse_sem).wait_send()
-    moved_pages = recv_ref.at[pl.ds(CAP, (NDP - 1) * CAP)]
+    moved_pages = comb_ref.at[pl.ds(SLOTS + CAP, (NDP - 1) * CAP)]
     pltpu.make_async_remote_copy(
         src_ref=moved_pages, dst_ref=moved_pages, send_sem=page_send.at[0], recv_sem=page_recv.at[0],
         device_id=(me, ts[1]), device_id_type=MESH,
     ).wait_recv()
 
 
-def place_kernel(code_ref, local_ref, recv_ref, proj_ref, new_ref, out_ref, sems, out_sem):
-    result = pltpu.make_async_copy(proj_ref, out_ref, out_sem)
-    result.start()
-
-    def put(s, carry):
-        code = code_ref[0, s]
-
-        @pl.when(code == 0)
-        def _():
-            pltpu.make_async_copy(local_ref.at[s], new_ref.at[s], sems.at[s]).start()
-
-        @pl.when(code > 0)
-        def _():
-            pltpu.make_async_copy(recv_ref.at[code - 1], new_ref.at[s], sems.at[s]).start()
-
-        return carry
-
-    lax.fori_loop(0, SLOTS, put, 0)
-
-    def drain(s, carry):
-        pltpu.make_async_copy(local_ref.at[0], new_ref.at[0], sems.at[s]).wait()
-        return carry
-
-    lax.fori_loop(0, SLOTS, drain, 0)
-    result.wait()
+def place_kernel(code_ref, comb_ref, proj_ref, new_ref, out_ref, sems, out_sem):
+    copies = []
+    for s in range(SLOTS):
+        copies.append(pltpu.make_async_copy(comb_ref.at[code_ref[0, s]], new_ref.at[s], sems.at[s]))
+        copies[-1].start()
+    copies.append(pltpu.make_async_copy(proj_ref, out_ref, out_sem))
+    copies[-1].start()
+    for copy in copies:
+        copy.wait()
 
 
 def body(query, kv_pages, move_plan, move_count, block_table, seq_lens, out_weight):
-    kv = kv_pages.reshape(SLOTS, *PAGE)
+    def in_hbm(x):
+        return pltpu.with_memory_space_constraint(x, pltpu.HBM)
+
+    kv = in_hbm(kv_pages.reshape(SLOTS, *PAGE))
+    table = in_hbm(block_table)
+    lens = in_hbm(seq_lens)
     dma = pltpu.SemaphoreType.DMA
     i32 = jnp.int32
     columns = out_weight.shape[1]
     seqs = NDP * SEQ_DEV
-    send, tags, meta = pl.pallas_call(
-        pack_kernel,
-        name="pack",
-        out_shape=[pltpu.VMEM((NDP * CAP, *PAGE), bf16), pltpu.VMEM((NDP, 1, 128), i32), pltpu.VMEM((1, 1, 128), i32)],
-        in_specs=[sspec(), sspec(), sspec(), sspec(), hspec()],
-        out_specs=[vspec()] * 3,
-        scratch_shapes=[pltpu.SMEM((NDP,), i32), dma((MOVES,))],
-        compiler_params=pltpu.CompilerParams(vmem_limit_bytes=VMEM_LIMIT),
-    )(jnp.transpose(move_plan, (1, 0, 2)), move_count, block_table, seq_lens, kv)
-    local, recv, code, projected = pl.pallas_call(
+    comb, code, projected = pl.pallas_call(
         step_kernel,
         name="step",
         out_shape=[
-            pltpu.VMEM((SLOTS, *PAGE), bf16),
-            pltpu.VMEM((NDP * CAP, *PAGE), bf16),
+            pltpu.VMEM((SLOTS + NDP * CAP, *PAGE), bf16),
             pltpu.VMEM((1, 128), i32),
             pltpu.VMEM((seqs, columns), bf16),
         ],
-        in_specs=[sspec(), sspec(), vspec(), vspec(), vspec(), vspec(), vspec(), hspec()],
-        out_specs=[vspec()] * 4,
+        in_specs=[sspec()] + [hspec()] * 6,
+        out_specs=[vspec()] * 3,
         scratch_shapes=[
+            pltpu.VMEM((3, 1, MOVES), i32),
+            pltpu.SMEM((SEQ_DEV, BLOCKS), i32),
+            pltpu.SMEM((SEQ_DEV,), i32),
+            pltpu.VMEM((SEQ_DEV * HEADS, HD), bf16),
+            pltpu.VMEM(out_weight.shape, bf16),
+            pltpu.VMEM((SLOTS, *PAGE), bf16),
+            pltpu.VMEM((NDP * CAP, *PAGE), bf16),
+            pltpu.VMEM((NDP, 1, 128), i32),
+            pltpu.VMEM((1, 1, 128), i32),
             pltpu.VMEM((NDP, 1, 128), i32),
             pltpu.VMEM((NDP, 1, 128), i32),
             pltpu.VMEM((NDP, SEQ_DEV * HEADS, HD), bf16),
@@ -455,7 +451,7 @@
             pltpu.VMEM((NDP, SEQ_DEV, HEADS * HD), bf16),
             pltpu.VMEM((seqs, columns), f32),
             pltpu.VMEM((NT, seqs // NT, columns), f32),
-            dma(()), dma((WINDOW,)), dma((1,)), dma((2,)), dma((2,)), dma((2,)), dma((2,)),
+            dma((5,)), dma((2,)), dma((WINDOW,)), dma((1,)), dma((2,)), dma((2,)), dma((2,)), dma((2,)),
             dma((NZ,)), dma((NZ,)), dma((NDP,)), dma((NDP,)),
             dma((NZ,)), dma((NZ,)), dma((NDP,)), dma((NDP,)),
             dma((NT,)), dma((NT,)), dma((NT,)), dma((NT,)),
@@ -463,7 +459,7 @@
         compiler_params=pltpu.CompilerParams(
             collective_id=0, has_side_effects=True, vmem_limit_bytes=VMEM_LIMIT
         ),
-    )(block_table, seq_lens, send, tags, meta, query.reshape(SEQ_DEV * HEADS, HD), out_weight, kv)
+    )(move_count, in_hbm(jnp.transpose(move_plan, (1, 0, 2))), table, lens, in_hbm(query.reshape(SEQ_DEV * HEADS, HD)), in_hbm(out_weight), kv)
     new_pages, projected = pl.pallas_call(
         place_kernel,
         name="place",
@@ -471,11 +467,11 @@
             jax.ShapeDtypeStruct((SLOTS, *PAGE), bf16),
             jax.ShapeDtypeStruct((seqs, columns), bf16),
         ],
-        in_specs=[sspec(), vspec(), vspec(), vspec()],
+        in_specs=[sspec(), vspec(), vspec()],
         out_specs=[hspec(), hspec()],
         scratch_shapes=[dma((SLOTS,)), dma(())],
         compiler_params=pltpu.CompilerParams(vmem_limit_bytes=VMEM_LIMIT),
-    )(code, local, recv, projected)
+    )(code, comb, projected)
     return new_pages.reshape(kv_pages.shape), projected
 
 

time: 135 us -> 120 us (0.89)
  Pallas kernels: 127 us -> 118 us
  local copies, waits for them, and re-layouts: 6.41 us -> 0 us
    pallas_call x2 -> x1, Pallas kernels: 123 us -> 114 us  [body(): pl.pallas_call(step_kernel, name='step', out_shape=[pltpu.VMEM((SLOTS + N...]
    unnamed x16 -> x0, local copies, waits for them, and re-layouts: 6.41 us -> none
where the time goes in v3:
time: 120 us; the launch traced here: 119 us
  Pallas kernels  118 us (98%)
  between operations  1.29 us (1%)
    pallas_call x1, Pallas kernels, body(): pl.pallas_call(step_kernel, name='step', out_shape=[pltpu.VMEM((SLOTS + N...  114 us
    pallas_call x1, Pallas kernels, body(): pl.pallas_call(place_kernel, name='place', out_shape=[jax.ShapeDtypeStruc...  3.81 us

profile of v3, /device:TPU:1, one launch (start us, length us, event | category | flops | bytes accessed | tf_op | source)
XLA Modules:
  0.0 119.1 jit_solution(17555442126417802230)
XLA Ops:
  1.3 114.0 %step.1 = (bf16[152,2,128,128]{3,2,1,0:T(8,128)(2,1)S(1)}, s32[1,128]{1,0:T(1,128)S(1)}, bf16[256,256]{1,0:T(8,128)(2,1)S(1)}) custom-call(s32[1]{0:T(128)S(6)} %copy.10.count_ref, s32[3,1,48]{2,1,0:T(1,128)} %bitcast.8, s32[8,8]{1,0:T(8,128)} %table_hbm.1, s32[8]{0:T(128)} %lens_hbm.1, bf16[64,128]{1,0:T(8,128)(2,1)} %bitcast.7, bf16[1024,256]{1,0:T(8,128)(2,1)} %w_hbm.1, ...), custom_call_target="tpu_custom_call" | custom-call | tf_op jit(solution)/shard_map/step/pallas_call | solution.py:418
  115.3 3.8 %place.1 = (bf16[88,2,128,128]{3,2,1,0:T(8,128)(2,1)}, bf16[256,256]{1,0:T(8,128)(2,1)}) custom-call(s32[1,128]{1,0:T(1,128)S(1)} %get-tuple-element.7.code_ref, bf16[152,2,128,128]{3,2,1,0:T(8,128)(2,1)S(1)} %get-tuple-element.8.comb_ref, bf16[256,256]{1,0:T(8,128)(2,1)S(1)} %get-tuple-element.9.proj_ref), custom_call_target="tpu_custom_call" | custom-call | tf_op jit(solution)/shard_map/place/pallas_call | solution.py:463

commit v4 on v3

--- a/solution.py
+++ b/solution.py
@@ -19,7 +19,8 @@
 NT = 8
 SEQ_DEV = 8
 HEADS = 8
-WINDOW = 16
+WINDOW = 12
+TAG_LANE = SEQ_DEV * BLOCKS + SEQ_DEV
 NEG = -1e30
 SCALE = 1.0 / math.sqrt(HD)
 MESH = pl.DeviceIdType.MESH
@@ -49,8 +50,9 @@
 def step_kernel(
     count_ref, plan_hbm, table_hbm, lens_hbm, query_hbm, w_hbm, kv_ref,
     comb_ref, code_ref, out_ref,
-    plan_ref, table_ref, lens_ref, query_ref, w_ref, local_ref, send_ref, tags_ref, meta_ref, got, metas, qall, src_seq, src_end, arr_seq, part, lse, apart, alse, wide, mixed, att, gath, proj, red,
-    in_sems, load_sem, page_send, page_recv, tag_sem, meta_sem, part_sem, lse_sem,
+    plan_ref, table_ref, lens_ref, query_ref, w_ref, local_ref, send_ref, tags_ref,
+    got, qall, src_seq, src_end, arr_seq, part, lse, apart, alse, wide, mixed, att, gath, proj, red,
+    in_sems, load_sem, page_send, page_recv, tag_sem, part_sem, lse_sem,
     qz_send, qz_recv, qy_send, qy_recv, z_send, z_recv, y_send, y_recv, r_send, r_recv, o_send, o_recv,
 ):
     me = lax.axis_index("dp")
@@ -59,21 +61,21 @@
     zs = [lax.rem(z + d, NZ) for d in range(NZ)]
     ys = [lax.rem(y + d, NY) for d in range(NY)]
     ts = [lax.rem(t + d, NT) for d in range(NT)]
-    fetch = [
-        pltpu.make_async_copy(a, b, in_sems.at[i])
-        for i, (a, b) in enumerate(
-            [(plan_hbm, plan_ref), (query_hbm, query_ref), (table_hbm, table_ref), (lens_hbm, lens_ref), (w_hbm, w_ref)]
-        )
-    ]
-    load = pltpu.make_async_copy(kv_ref, local_ref, load_sem.at[0])
-    keep = pltpu.make_async_copy(kv_ref, comb_ref.at[pl.ds(0, SLOTS)], load_sem.at[1])
-    for copy in fetch + [load, keep]:
-        copy.start()
     bar = pltpu.get_barrier_semaphore()
     order = sorted([s for s in SHIFTS if s != (0, 0)], key=lambda s: -far(s))
     peers = [(ys[dy] * NZ + zs[dz], t) for dy, dz in order] + [(me, ts[d]) for d in range(1, NT)]
     for peer in peers:
         pl.semaphore_signal(bar, inc=1, device_id=peer, device_id_type=MESH)
+    fetch = [
+        pltpu.make_async_copy(a, b, in_sems.at[i])
+        for i, (a, b) in enumerate(
+            [(plan_hbm, plan_ref), (query_hbm, query_ref), (table_hbm, table_ref), (lens_hbm, lens_ref), (w_hbm, w_ref)]
+        )
+    ]
+    load = pltpu.make_async_copy(kv_ref, local_ref, load_sem.at[0])
+    keep = pltpu.make_async_copy(kv_ref, comb_ref.at[pl.ds(0, SLOTS)], load_sem.at[1])
+    for copy in fetch[:4] + [load]:
+        copy.start()
 
     i32 = jnp.int32
     for copy in fetch[:4]:
@@ -91,24 +93,25 @@
     shift = (((goes >> 3) - y) & (NY - 1)) * NZ + ((goes - z) & (NZ - 1))
     row = jnp.where(iota((1, MOVES), 1) < count_ref[0], shift * CAP + rank, -1)
     lane = iota((NDP, 128), 1)
-    tags = jnp.full((NDP, 128), -1, i32)
-    source = []
-    for c in range(CAP):
-        hit = jnp.broadcast_to(row, (NDP, MOVES)) == iota((NDP, MOVES), 0) * CAP + c
-        source.append(
-            jnp.sum(jnp.where(hit, jnp.broadcast_to(plan_ref[0], (NDP, MOVES)), 0), axis=1, keepdims=True)
-        )
-        slot = jnp.sum(jnp.where(hit, jnp.broadcast_to(plan_ref[2], (NDP, MOVES)) + 1, 0), axis=1, keepdims=True) - 1
-        tags = jnp.where(lane == c, slot, tags)
-    tags_ref[...] = tags.reshape(NDP, 1, 128)
     lane1 = iota((1, 128), 1)
     meta = jnp.full((1, 128), -2, i32)
     for s in range(SEQ_DEV):
         for b in range(BLOCKS):
             meta = jnp.where(lane1 == s * BLOCKS + b, table_ref[s, b], meta)
         meta = jnp.where(lane1 == SEQ_DEV * BLOCKS + s, lens_ref[s], meta)
-    meta_ref[0] = meta
+    tags = jnp.broadcast_to(meta, (NDP, 128))
+    source = []
+    for c in range(CAP):
+        hit = jnp.broadcast_to(row, (NDP, MOVES)) == iota((NDP, MOVES), 0) * CAP + c
+        source.append(
+            jnp.sum(jnp.where(hit, jnp.broadcast_to(plan_ref[0], (NDP, MOVES)), 0), axis=1, keepdims=True)
+        )
+        slot = jnp.sum(jnp.where(hit, jnp.broadcast_to(plan_ref[2], (NDP, MOVES)) + 1, 0), axis=1, keepdims=True) - 1
+        tags = jnp.where(lane == TAG_LANE + c, slot, tags)
+    tags_ref[...] = tags.reshape(NDP, 1, 128)
     load.wait()
+    keep.start()
+    fetch[4].start()
 
     def take(c, k):
         send_ref[k * CAP + c] = local_ref[source[c][k, 0]]
@@ -148,39 +151,45 @@
                 remote(send_ref.at[row], comb_ref.at[SLOTS + row], page_send.at[i % WINDOW], page_recv.at[0], to(s))
             )
 
-    z_order = sorted(range(1, NZ), key=lambda d: -min(d, NZ - d))
-    z_near = sorted(range(1, NZ), key=lambda d: min(d, NZ - d))
-
-    def gather_start(own_ref, buf, zsend, zrecv, ysend, yrecv):
-        along_z = {d: remote(own_ref, buf.at[me], zsend.at[d], zrecv.at[d], (y * NZ + zs[d], t)) for d in z_order}
+    relays = {2: (1, 2), 6: (7,)}
+
+    def gather_start(own_ref, buf, zsend, zrecv, ysend, yrecv, sign):
+        along_z = {}
+        for d in (2, 6, 1, 7):
+            e = d * sign % NZ
+            along_z[e] = remote(own_ref, buf.at[me], zsend.at[e], zrecv.at[e], (y * NZ + zs[e], t))
         along_y = [
             remote(own_ref, buf.at[me], ysend.at[d], yrecv.at[d], (ys[d] * NZ + z, t)) for d in (2, 1, 3)
         ]
         buf[me] = own_ref[...]
         return along_z, along_y
 
-    def gather_forward(along_z, along_y, buf, ysend, yrecv, pumps):
-        for e in z_near:
+    def gather_forward(along_z, along_y, buf, zsend, zrecv, ysend, yrecv, sign, pumps):
+        for d in (2, 6, 1, 7, 3, 5, 4):
+            e = d * sign % NZ
             along_z[e].wait_recv()
             held = y * NZ + lax.rem(z - e + NZ, NZ)
-            for d in (2, 1, 3):
-                n = e * NY + d
+            for step in relays.get(d, ()):
+                there = (d + step) * sign % NZ
+                along_z[there] = remote(
+                    buf.at[held], buf.at[held], zsend.at[there], zrecv.at[there],
+                    (y * NZ + zs[step * sign % NZ], t),
+                )
+            for d_y in (2, 1, 3):
+                n = e * NY + d_y
                 along_y.append(
-                    remote(buf.at[held], buf.at[held], ysend.at[n], yrecv.at[n], (ys[d] * NZ + z, t))
+                    remote(buf.at[held], buf.at[held], ysend.at[n], yrecv.at[n], (ys[d_y] * NZ + z, t))
                 )
             pump(pumps)
 
-    q_z, q_y = gather_start(query_ref, qall, qz_send, qz_recv, qy_send, qy_recv)
+    q_z, q_y = gather_start(query_ref, qall, qz_send, qz_recv, qy_send, qy_recv, 1)
     small = []
     for s in order:
-        back = ((NY - s[0]) % NY, (NZ - s[1]) % NZ)
         small.append(remote(tags_ref.at[at(s)], got.at[at(s)], tag_sem.at[0], tag_sem.at[1], to(s)))
-        small.append(remote(meta_ref.at[0], metas.at[at(back)], meta_sem.at[0], meta_sem.at[1], to(s)))
     got[0] = tags_ref[0]
-    metas[0] = meta_ref[0]
     pump(WINDOW)
     comb_ref[SLOTS : SLOTS + CAP] = send_ref[0:CAP]
-    gather_forward(q_z, q_y, qall, qy_send, qy_recv, 1)
+    gather_forward(q_z, q_y, qall, qz_send, qz_recv, qy_send, qy_recv, 1, 1)
 
     def all_of(buf, sems):
         return pltpu.make_async_remote_copy(
@@ -193,24 +202,23 @@
         )
 
     all_of(got, tag_sem).wait_recv()
-    all_of(metas, meta_sem).wait_recv()
     lane_f = lane.astype(f32)
     first = lane < SEQ_DEV * BLOCKS
     seq_f = (lane // BLOCKS).astype(f32)
     block_f = (lane % BLOCKS).astype(f32)
     device_f = lax.broadcasted_iota(jnp.int32, (NDP, 128), 0).astype(f32)
-    mine = metas[0]
+    mine = got[0]
     moved = jnp.zeros((1, 128), f32)
     code = lane1.astype(f32)
     sent_tags = tags_ref[...].reshape(NDP, 128)
     got_tags = got[...].reshape(NDP, 128)
-    tables = metas[...].reshape(NDP, 128)
+    tables = jnp.concatenate([got[at(((NY - dy) % NY, (NZ - dz) % NZ))] for dy, dz in SHIFTS], axis=0)
 
     def spread(column):
         return jnp.broadcast_to(column, (NDP, 128)).reshape(NDP, 1, 128)
 
     for c in range(CAP):
-        tag = sent_tags[:, c : c + 1]
+        tag = sent_tags[:, TAG_LANE + c : TAG_LANE + c + 1]
         hit = (tables == tag) & first & (tag >= 0)
         found = jnp.sum(jnp.where(hit, 1.0, 0.0), axis=1, keepdims=True)
         seq = jnp.sum(jnp.where(hit, seq_f, 0.0), axis=1, keepdims=True)
@@ -220,7 +228,7 @@
         )
         src_seq[c] = spread(jnp.where(found > 0, seq, -1.0))
         src_end[c] = spread(ends - block * BLOCK)
-        tag = got_tags[:, c : c + 1]
+        tag = got_tags[:, TAG_LANE + c : TAG_LANE + c + 1]
         hit = (mine == tag) & first & (tag >= 0)
         found = jnp.sum(jnp.where(hit, 1.0, 0.0), axis=1, keepdims=True)
         seq = jnp.sum(jnp.where(hit, seq_f, 0.0), axis=1, keepdims=True)
@@ -349,9 +357,9 @@
         [mixed[pl.ds(h, SEQ_DEV, stride=HEADS), :] for h in range(HEADS)], axis=1
     ).astype(bf16)
 
-    along_z, along_y = gather_start(att, gath, z_send, z_recv, y_send, y_recv)
+    along_z, along_y = gather_start(att, gath, z_send, z_recv, y_send, y_recv, -1)
     pump(4)
-    gather_forward(along_z, along_y, gath, y_send, y_recv, 1)
+    gather_forward(along_z, along_y, gath, z_send, z_recv, y_send, y_recv, -1, 1)
     pump(2)
     for copy in along_y:
         copy.wait_recv()
@@ -383,7 +391,6 @@
     for copy in list(q_z.values()) + q_y + list(along_z.values()) + along_y + sums + outs:
         copy.wait_send()
     all_of(got, tag_sem).wait_send()
-    all_of(metas, meta_sem).wait_send()
     all_of(part, part_sem).wait_send()
     all_of(lse, lse_sem).wait_send()
     moved_pages = comb_ref.at[pl.ds(SLOTS + CAP, (NDP - 1) * CAP)]
@@ -434,8 +441,6 @@
             pltpu.VMEM((SLOTS, *PAGE), bf16),
             pltpu.VMEM((NDP * CAP, *PAGE), bf16),
             pltpu.VMEM((NDP, 1, 128), i32),
-            pltpu.VMEM((1, 1, 128), i32),
-            pltpu.VMEM((NDP, 1, 128), i32),
             pltpu.VMEM((NDP, 1, 128), i32),
             pltpu.VMEM((NDP, SEQ_DEV * HEADS, HD), bf16),
             pltpu.VMEM((CAP, NDP, 1, 128), f32),
@@ -451,7 +456,7 @@
             pltpu.VMEM((NDP, SEQ_DEV, HEADS * HD), bf16),
             pltpu.VMEM((seqs, columns), f32),
             pltpu.VMEM((NT, seqs // NT, columns), f32),
-            dma((5,)), dma((2,)), dma((WINDOW,)), dma((1,)), dma((2,)), dma((2,)), dma((2,)), dma((2,)),
+            dma((5,)), dma((2,)), dma((WINDOW,)), dma((1,)), dma((2,)), dma((2,)), dma((2,)),
             dma((NZ,)), dma((NZ,)), dma((NDP,)), dma((NDP,)),
             dma((NZ,)), dma((NZ,)), dma((NDP,)), dma((NDP,)),
             dma((NT,)), dma((NT,)), dma((NT,)), dma((NT,)),

time: 120 us -> 120 us (level)
  no operation moved by 1% of the time
where the time goes in v4:
time: 120 us
  Pallas kernels  118 us (98%)
  between operations  1.29 us (1%)
    pallas_call x1, Pallas kernels, body(): pl.pallas_call(step_kernel, name='step', out_shape=[pltpu.VMEM((SLOTS + N...  114 us
    pallas_call x1, Pallas kernels, body(): pl.pallas_call(place_kernel, name='place', out_shape=[jax.ShapeDtypeStruc...  3.81 us

profile of v4, /device:TPU:1, one launch (start us, length us, event | category | flops | bytes accessed | tf_op | source)
XLA Modules:
  0.0 119.5 jit_solution(12683079746478754244)
XLA Ops:
  1.3 114.4 %step.1 = (bf16[152,2,128,128]{3,2,1,0:T(8,128)(2,1)S(1)}, s32[1,128]{1,0:T(1,128)S(1)}, bf16[256,256]{1,0:T(8,128)(2,1)S(1)}) custom-call(s32[1]{0:T(128)S(6)} %copy.10.count_ref, s32[3,1,48]{2,1,0:T(1,128)} %bitcast.8, s32[8,8]{1,0:T(8,128)} %table_hbm.1, s32[8]{0:T(128)} %lens_hbm.1, bf16[64,128]{1,0:T(8,128)(2,1)} %bitcast.7, bf16[1024,256]{1,0:T(8,128)(2,1)} %w_hbm.1, ...), custom_call_target="tpu_custom_call" | custom-call | tf_op jit(solution)/shard_map/step/pallas_call | solution.py:425
  115.7 3.8 %place.1 = (bf16[88,2,128,128]{3,2,1,0:T(8,128)(2,1)}, bf16[256,256]{1,0:T(8,128)(2,1)}) custom-call(s32[1,128]{1,0:T(1,128)S(1)} %get-tuple-element.7.code_ref, bf16[152,2,128,128]{3,2,1,0:T(8,128)(2,1)S(1)} %get-tuple-element.8.comb_ref, bf16[256,256]{1,0:T(8,128)(2,1)S(1)} %get-tuple-element.9.proj_ref), custom_call_target="tpu_custom_call" | custom-call | tf_op jit(solution)/shard_map/place/pallas_call | solution.py:468

commit v5 on v4

--- a/solution.py
+++ b/solution.py
@@ -300,7 +300,7 @@
         return carry
 
     for g in range(4):
-        lax.fori_loop(g * NZ, (g + 1) * NZ, partial, 0)
+        lax.fori_loop(g * NZ, (g + 1) * NZ, partial, 0, unroll=4)
         for dz in range(NZ):
             if (g, dz) != (0, 0):
                 k = at((g, dz))
@@ -328,7 +328,7 @@
                 tops[s] = jnp.where(seq == s, jnp.maximum(tops[s], full), tops[s])
         return tuple(tops)
 
-    tops = lax.fori_loop(0, NDP, widen, tuple(wide[s] for s in range(SEQ_DEV)))
+    tops = lax.fori_loop(0, NDP, widen, tuple(wide[s] for s in range(SEQ_DEV)), unroll=4)
     start = []
     for s in range(SEQ_DEV):
         w = jnp.exp(wide[s] - tops[s])
@@ -349,7 +349,7 @@
         return tuple(dens), tuple(nums)
 
     dens, nums = lax.fori_loop(
-        0, NDP, merge, (tuple(a for a, _ in start), tuple(b for _, b in start))
+        0, NDP, merge, (tuple(a for a, _ in start), tuple(b for _, b in start)), unroll=4
     )
     for s in range(SEQ_DEV):
         mixed[s * HEADS : (s + 1) * HEADS, :] = nums[s] / dens[s]

time: 120 us -> 116 us (0.967)
  Pallas kernels: 118 us -> 114 us
    pallas_call x1, Pallas kernels: 114 us -> 111 us  [body(): pl.pallas_call(step_kernel, name='step', out_shape=[pltpu.VMEM((SLOTS + N...]
where the time goes in v5:
time: 116 us
  Pallas kernels  114 us (98%)
  between operations  1.29 us (1%)
    pallas_call x1, Pallas kernels, body(): pl.pallas_call(step_kernel, name='step', out_shape=[pltpu.VMEM((SLOTS + N...  111 us
    pallas_call x1, Pallas kernels, body(): pl.pallas_call(place_kernel, name='place', out_shape=[jax.ShapeDtypeStruc...  3.81 us

profile of v5, /device:TPU:1, one launch (start us, length us, event | category | flops | bytes accessed | tf_op | source)
XLA Modules:
  0.0 115.8 jit_solution(12638469490346758189)
XLA Ops:
  1.3 110.7 %step.1 = (bf16[152,2,128,128]{3,2,1,0:T(8,128)(2,1)S(1)}, s32[1,128]{1,0:T(1,128)S(1)}, bf16[256,256]{1,0:T(8,128)(2,1)S(1)}) custom-call(s32[1]{0:T(128)S(6)} %copy.10.count_ref, s32[3,1,48]{2,1,0:T(1,128)} %bitcast.8, s32[8,8]{1,0:T(8,128)} %table_hbm.1, s32[8]{0:T(128)} %lens_hbm.1, bf16[64,128]{1,0:T(8,128)(2,1)} %bitcast.7, bf16[1024,256]{1,0:T(8,128)(2,1)} %w_hbm.1, ...), custom_call_target="tpu_custom_call" | custom-call | tf_op jit(solution)/shard_map/step/pallas_call | solution.py:425
  112.0 3.8 %place.1 = (bf16[88,2,128,128]{3,2,1,0:T(8,128)(2,1)}, bf16[256,256]{1,0:T(8,128)(2,1)}) custom-call(s32[1,128]{1,0:T(1,128)S(1)} %get-tuple-element.7.code_ref, bf16[152,2,128,128]{3,2,1,0:T(8,128)(2,1)S(1)} %get-tuple-element.8.comb_ref, bf16[256,256]{1,0:T(8,128)(2,1)S(1)} %get-tuple-element.9.proj_ref), custom_call_target="tpu_custom_call" | custom-call | tf_op jit(solution)/shard_map/place/pallas_call | solution.py:468
